TPU v7x, 32 devices: a whole 2x2x4 slice. The times are simulated.
32 devices in a mesh: gx: 2 (over x), gy: 4 (over y, core), gz: 4 (over z).
Axes of the slice: x: 2, y: 2, z: 4, core: 2. Of those that a mesh axis runs over, the one named last changes fastest.
Arguments:
- metric_pert: float32 [6, 32, 64, 512], P(None, 'gx', 'gy', 'gz'), may hold values from -1.8 to 1.8
- curvature: float32 [6, 32, 64, 512], P(None, 'gx', 'gy', 'gz'), may hold values from -6 to 6
- interp_weights: bfloat16 [2, 4, 32, 64, 4096], P('gx', 'gy', 'gz'), may hold values from -0.09375 to 0.09375
- point_ids: int32 [2, 4, 32, 64], P('gx', 'gy', 'gz'), may hold values from 0 to 6144, as said below
- theta: float32 [6144], replicated, may hold values from 0.05 to 3.09
- phi: float32 [6144], replicated, may hold values from -3.140625 to 3.140625
Outputs:
- psi4_field: bfloat16 [2, 32, 64, 512], P(None, 'gx', 'gy', 'gz')
- modes: float32 [3, 2, 77], replicated
Inputs may be any that keep to these rules, and one draw needn't show every extreme that they name: `point_ids`: the grid is a window of the extraction region that the spheres cross. A live entry names a sphere point; the value 6144 marks an empty slot, and each list holds its live entries first. The points of sphere s lie in the 9 consecutive block layers along the third dimension that begin at layer s * 10; each point belongs to one column (bx, by) and is listed in exactly two blocks of that column that are adjacent along the third dimension. Some block's list is full, every listing block holds at least 32 live entries, and blocks outside these layers list no point.
All inputs are finite; a program needn't handle non-finite values.
Results may differ from a plain program's by a relative error of at most 0.0032.
Values sent between devices are 32-bit elements; how exact they have to be, the bound alone decides.
No kernel may reach another device: no remote copies, remote signals or barrier semaphores. Data moves between devices by JAX's collectives and lax.ppermute only.
A program may use at most 64 MiB of HBM per device.

v0:
```python
import math

import jax
import jax.numpy as jnp
import numpy as np
from jax import lax
from jax.sharding import PartitionSpec as P

BLK = 16
PB = 64
PTS = 2048
SPHERES = 3
LMAX = 8


PAIRS = [[0, 1, 2], [1, 3, 4], [2, 4, 5]]


def padded_2(cells, sides, width):
    for axis, dim in sides:
        count = lax.axis_size(axis)
        ends = count - 1
        head = lax.slice_in_dim(cells, 0, width, axis=dim)
        tail = lax.slice_in_dim(cells, cells.shape[dim] - width, cells.shape[dim], axis=dim)
        cells = jnp.concatenate(
            [
                lax.ppermute(tail, axis, [(i, (i + 1) % count) for i in range(ends)]),
                cells,
                lax.ppermute(head, axis, [((i + 1) % count, i) for i in range(ends)]),
            ],
            axis=dim,
        )
    return cells


def build_table(degree_max):
    width = 2 * degree_max + 1
    columns = []
    orders = []
    for degree in range(2, degree_max + 1):
        for order in range(-degree, degree + 1):
            column = np.zeros(width * width)
            lead = (-1.0) ** order * math.sqrt(
                math.factorial(degree + order)
                * math.factorial(degree - order)
                * (2 * degree + 1)
                / (4.0 * math.pi * math.factorial(degree - 2) * math.factorial(degree + 2))
            )
            for step in range(0, degree + 3):
                lower = step - 2 - order
                if lower >= 0 and lower <= degree - 2:
                    value = (
                        lead
                        * math.comb(degree + 2, step)
                        * math.comb(degree - 2, lower)
                        * (-1.0) ** (degree - step + 2)
                    )
                    expo = 2 * step - 2 - order
                    column[expo * width + (2 * degree - expo)] += value
            columns.append(column)
            orders.append(order)
    return (np.stack(columns, 1), np.array(orders))


def project(sphere_vals, theta, phi, member):
    table, orders = build_table(LMAX)
    width = 2 * LMAX + 1
    cosine = jnp.cos(theta * 0.5)
    sine = jnp.sin(theta * 0.5)
    cos_pow = jnp.stack([cosine**power for power in range(width)], 1)
    sin_pow = jnp.stack([sine**power for power in range(width)], 1)
    grid_pow = (cos_pow[:, :, None] * sin_pow[:, None, :]).reshape(theta.shape[0], width * width)
    amplitude = jnp.dot(grid_pow, jnp.asarray(table, jnp.float32), precision=lax.Precision.HIGHEST)
    angle_m = phi[:, None] * jnp.asarray(orders, jnp.float32)[None, :]
    y_real = amplitude * jnp.cos(angle_m)
    y_imag = amplitude * jnp.sin(angle_m)
    left_re = member * sphere_vals[0][None, :]
    left_im = member * sphere_vals[1][None, :]
    highest = lax.Precision.HIGHEST
    real = jnp.dot(left_re, y_real, precision=highest) + jnp.dot(left_im, y_imag, precision=highest)
    imag = jnp.dot(left_im, y_real, precision=highest) - jnp.dot(left_re, y_imag, precision=highest)
    return jnp.stack([real, imag], 1) * (4.0 * math.pi / PTS)


def frame_terms(x_coord, y_coord, z_coord):
    x_full = x_coord[:, None, None]
    y_full = y_coord[None, :, None]
    z_full = z_coord[None, None, :]
    radial_xy = jnp.sqrt(x_full * x_full + y_full * y_full)
    radius = jnp.sqrt(radial_xy * radial_xy + z_full * z_full)
    cos_phi = x_full / radial_xy
    sin_phi = y_full / radial_xy
    cos_theta = z_full / radius
    sin_theta = radial_xy / radius
    e_theta = [cos_theta * cos_phi, cos_theta * sin_phi, -sin_theta]
    e_phi = [-sin_phi, cos_phi, 0.0 * cos_phi]
    return (e_theta, e_phi)


def weyl_scalar(padded, x_coord, y_coord, z_coord):
    extent = [x_coord.shape[0], y_coord.shape[0], z_coord.shape[0]]

    def moved(comp, axis, offset):
        index = [slice(2, 2 + count) for count in extent]
        index[axis] = slice(2 + offset, 2 + offset + extent[axis])
        return padded[comp][tuple(index)]

    def first(comp, axis):
        return (
            moved(comp, axis, -2)
            - 8.0 * moved(comp, axis, -1)
            + 8.0 * moved(comp, axis, 1)
            - moved(comp, axis, 2)
        ) / 12.0

    def second(comp, axis):
        return (
            -moved(comp, axis, -2)
            + 16.0 * moved(comp, axis, -1)
            - 30.0 * moved(comp, axis, 0)
            + 16.0 * moved(comp, axis, 1)
            - moved(comp, axis, 2)
        ) / 12.0

    kval = [moved(6 + comp, 0, 0) for comp in range(6)]
    trace = kval[0] + kval[3] + kval[5]
    electric = {}
    for row in range(3):
        for col in range(row, 3):
            comp = PAIRS[row][col]
            laplace = second(comp, 0) + second(comp, 1) + second(comp, 2)
            square = (
                kval[PAIRS[row][0]] * kval[PAIRS[0][col]]
                + kval[PAIRS[row][1]] * kval[PAIRS[1][col]]
                + kval[PAIRS[row][2]] * kval[PAIRS[2][col]]
            )
            value = -0.5 * laplace + trace * kval[comp] - square
            electric[row, col] = value
            electric[col, row] = value
    deriv = [[first(6 + comp, axis) for comp in range(6)] for axis in range(3)]
    curl = {}
    for row in range(3):
        one = (row + 1) % 3
        two = (row + 2) % 3
        for col in range(3):
            curl[row, col] = deriv[one][PAIRS[two][col]] - deriv[two][PAIRS[one][col]]
    e_theta, e_phi = frame_terms(x_coord, y_coord, z_coord)
    real = 0.0
    imag = 0.0
    for row in range(3):
        for col in range(3):
            magnetic = 0.5 * (curl[row, col] + curl[col, row])
            plus = 0.5 * (e_theta[row] * e_theta[col] - e_phi[row] * e_phi[col])
            cross = 0.5 * (e_theta[row] * e_phi[col] + e_phi[row] * e_theta[col])
            real = real + electric[row, col] * plus - magnetic * cross
            imag = imag - electric[row, col] * cross - magnetic * plus
    return jnp.stack([real, imag])


def shards(metric_pert, curvature, interp_weights, point_ids, theta, phi):
    fields = jnp.concatenate([metric_pert, curvature], 0)
    cells_x, cells_y, cells_z = (metric_pert.shape[1], metric_pert.shape[2], metric_pert.shape[3])
    whole_x = cells_x * lax.axis_size("gx")
    whole_y = cells_y * lax.axis_size("gy")
    whole_z = cells_z * lax.axis_size("gz")
    x_coord = (
        (lax.axis_index("gx") * cells_x + jnp.arange(cells_x)).astype(jnp.float32)
        + 0.5
        - whole_x / 2.0
    )
    y_coord = (
        (lax.axis_index("gy") * cells_y + jnp.arange(cells_y)).astype(jnp.float32)
        + 0.5
        - whole_y / 2.0
    )
    z_coord = (
        (lax.axis_index("gz") * cells_z + jnp.arange(cells_z)).astype(jnp.float32)
        + 0.5
        - whole_z / 2.0
    )
    padded = padded_2(fields, (("gx", 1), ("gy", 2), ("gz", 3)), 2)
    psi_local = weyl_scalar(padded, x_coord, y_coord, z_coord).astype(jnp.bfloat16)
    blocks_z = cells_z // BLK
    blocks = (
        psi_local.reshape(2, BLK, BLK, blocks_z, BLK)
        .transpose(3, 0, 1, 2, 4)
        .reshape(blocks_z, 2, BLK * BLK * BLK)
    )
    weights = interp_weights.reshape(blocks_z, PB, BLK * BLK * BLK)
    partial_value = jnp.einsum("bcn,bpn->bpc", blocks, weights, preferred_element_type=jnp.float32)
    slot_values = partial_value.reshape(-1, 2)
    point_list = point_ids.reshape(-1)
    total_points = SPHERES * PTS
    safe_list = jnp.minimum(point_list, total_points - 1)
    member = (point_list[None, :] // PTS == jnp.arange(SPHERES)[:, None]).astype(jnp.float32)
    local_modes = project(slot_values.T, theta[safe_list], phi[safe_list], member)
    modes = lax.psum(local_modes, ("gx", "gy", "gz"))
    return (psi_local, modes)


def solution(mesh):
    in_specs = (
        P(None, "gx", "gy", "gz"),
        P(None, "gx", "gy", "gz"),
        P("gx", "gy", "gz", None, None),
        P("gx", "gy", "gz", None),
        P(),
        P(),
    )
    out_specs = (P(None, "gx", "gy", "gz"), P())
    return jax.shard_map(shards, mesh=mesh, in_specs=in_specs, out_specs=out_specs, check_vma=False)
```

profile of v0, /device:TPU:0, one launch (start us, length us, event | category | flops | bytes accessed | tf_op | source)
XLA Modules:
  0.0 129.0 jit_solution(13485830494498539828)
XLA Ops:
  0.7 1.2 constant_dynamic-update-slice_fusion.1
  1.9 1.2 constant_dynamic-update-slice_fusion
  3.1 0.8 fusion.227
  3.9 4.9 %collective-permute-start = (f32[12,2,16,128]{3,2,1,0:T(8,128)}, f32[12,2,16,128]{3,2,1,0:T(8,128)S(1)}, u32[]{:S(2)}, u32[]{:S(2)}) collective-permute-start(f32[12,2,16,128]{3,2,1,0:T(8,128)} %get-tuple-element.43), channel_id=1, source_target_pairs={{0,16},{1,17},{2,18},{3,19},{4,20},{5,21},{6,22},{7,23},{8,24},{9,... | collective-permute-start | bytes 589832 | tf_op jit(solution)/shard_map/ppermute | solution.py:27
  8.8 1.3 %collective-permute-start.1 = (f32[12,2,16,128]{3,2,1,0:T(8,128)}, f32[12,2,16,128]{3,2,1,0:T(8,128)S(1)}, u32[]{:S(2)}, u32[]{:S(2)}) collective-permute-start(f32[12,2,16,128]{3,2,1,0:T(8,128)} %get-tuple-element.44), channel_id=1, source_target_pairs={{16,0},{17,1},{18,2},{19,3},{20,4},{21,5},{22,6},{23,7},{24,8},{25... | collective-permute-start | bytes 589832 | tf_op jit(solution)/shard_map/ppermute | solution.py:29
  10.8 3.1 %gather_fusion = f32[512]{0:T(512)S(1)} fusion(f32[6144]{0:T(1024)S(1)} %copy-done, s32[1024]{0:T(1024)S(1)} %pad_clamp_fusion), kind=kCustom, calls=%fused_computation | custom fusion | bytes 6144 | tf_op jit(solution)/shard_map/gather | solution.py:196
  14.4 0.7 fusion.167
  15.2 2.0 %collective-permute-done.1 = f32[12,2,16,128]{3,2,1,0:T(8,128)S(1)} collective-permute-done((f32[12,2,16,128]{3,2,1,0:T(8,128)}, f32[12,2,16,128]{3,2,1,0:T(8,128)S(1)}, u32[]{:S(2)}, u32[]{:S(2)}) %collective-permute-start.1) | collective-permute-done | bytes 196640 | tf_op jit(solution)/shard_map/ppermute | solution.py:29
  17.4 1.3 %collective-permute-start.2 = (f32[12,20,2,128]{3,2,1,0:T(2,128)S(1)}, f32[12,20,2,128]{3,2,1,0:T(2,128)S(1)}, u32[]{:S(2)}, u32[]{:S(2)}) collective-permute-start(f32[12,20,2,128]{3,2,1,0:T(2,128)S(1)} %get-tuple-element.41), channel_id=1, source_target_pairs={{0,4},{4,8},{8,12},{1,5},{5,9},{9,13},{2,6},{6,10},{10,14},{3,7},{... | collective-permute-start | bytes 737288 | tf_op jit(solution)/shard_map/ppermute | solution.py:27
  18.7 1.3 %collective-permute-start.3 = (f32[12,20,2,128]{3,2,1,0:T(2,128)S(1)}, f32[12,20,2,128]{3,2,1,0:T(2,128)S(1)}, u32[]{:S(2)}, u32[]{:S(2)}) collective-permute-start(f32[12,20,2,128]{3,2,1,0:T(2,128)S(1)} %get-tuple-element.42), channel_id=1, source_target_pairs={{4,0},{8,4},{12,8},{5,1},{9,5},{13,9},{6,2},{10,6},{14,10},{7,3},{... | collective-permute-start | bytes 737288 | tf_op jit(solution)/shard_map/ppermute | solution.py:29
  20.0 1.6 %fusion.229 = f32[512,77]{0,1:T(8,128)S(1)} fusion(f32[512,289]{0,1:T(8,128)S(1)} %mul.1636, f32[289,77]{1,0:T(8,128)} %constant.111.clone), kind=kOutput, calls=%fused_computation.419 | convolution fusion | flops 136722432 | bytes 838580 | tf_op jit(solution)/shard_map/dot_general | solution.py:73
  21.6 2.3 %collective-permute-done.3 = f32[12,20,2,128]{3,2,1,0:T(2,128)S(1)} collective-permute-done((f32[12,20,2,128]{3,2,1,0:T(2,128)S(1)}, f32[12,20,2,128]{3,2,1,0:T(2,128)S(1)}, u32[]{:S(2)}, u32[]{:S(2)}) %collective-permute-start.3) | collective-permute-done | bytes 245792 | tf_op jit(solution)/shard_map/ppermute | solution.py:29
  23.9 1.4 %pad_maximum_fusion.1 = f32[12,20,20,128]{3,2,1,0:T(8,128)S(1)} fusion(f32[12,20,2,128]{3,2,1,0:T(2,128)S(1)} %collective-permute-done.3, f32[12,2,16,128]{3,2,1,0:T(8,128)} %copy-done.2, f32[12,16,16,128]{3,2,1,0:T(8,128)S(1)} %constant_dynamic-update-slice_fusion, f32[12,2,16,128]{3,2,1,0:T(8,128)S(1)} %collective-permute-done, ...), kind=kLoop, calls=%fused_computation.5 | loop fusion | flops 2457600 | bytes 4915200 | tf_op jit(solution)/shard_map/concatenate | solution.py:25
  25.3 3.5 %fusion.226 = (f32[12,20,20,2]{3,2,1,0:T(8,128)}, f32[12,20,20,2]{3,2,1,0:T(8,128)}) fusion(f32[12,20,20,128]{3,2,1,0:T(8,128)S(1)} %pad_maximum_fusion.1), kind=kLoop, calls=%fused_computation.416 | loop fusion | bytes 153600 | tf_op jit(solution)/shard_map/slice | solution.py:24
  28.8 3.0 %copy.32 = f32[12,20,20,2]{2,3,1,0:T(2,128)S(1)} copy(f32[12,20,20,2]{3,2,1,0:T(8,128)} %get-tuple-element.39) | data formatting | bytes 76800
  31.8 3.5 %collective-permute-start.4 = (f32[12,20,20,2]{2,3,1,0:T(2,128)S(1)}, f32[12,20,20,2]{2,3,1,0:T(2,128)S(1)}, u32[]{:S(2)}, u32[]{:S(2)}) collective-permute-start(f32[12,20,20,2]{2,3,1,0:T(2,128)S(1)} %copy.32), channel_id=1, source_target_pairs={{0,1},{1,2},{2,3},{4,5},{5,6},{6,7},{8,9},{9,10},{10,11},{12,13},{... | collective-permute-start | bytes 115208 | tf_op jit(solution)/shard_map/ppermute | solution.py:27
  35.3 3.0 %copy.33 = f32[12,20,20,2]{2,3,1,0:T(2,128)S(1)} copy(f32[12,20,20,2]{3,2,1,0:T(8,128)} %get-tuple-element.40) | data formatting | bytes 76800
  38.4 1.5 %collective-permute-start.5 = (f32[12,20,20,2]{2,3,1,0:T(2,128)S(1)}, f32[12,20,20,2]{2,3,1,0:T(2,128)}, u32[]{:S(2)}, u32[]{:S(2)}) collective-permute-start(f32[12,20,20,2]{2,3,1,0:T(2,128)S(1)} %copy.33), channel_id=1, source_target_pairs={{1,0},{2,1},{3,2},{5,4},{6,5},{7,6},{9,8},{10,9},{11,10},{13,12},{... | collective-permute-start | bytes 115208 | tf_op jit(solution)/shard_map/ppermute | solution.py:29
  39.9 3.1 %gather_fusion.1 = f32[512]{0:T(512)S(1)} fusion(f32[6144]{0:T(1024)S(1)} %copy-done.1, s32[1024]{0:T(1024)S(1)} %pad_clamp_fusion), kind=kCustom, calls=%fused_computation.1 | custom fusion | bytes 6144 | tf_op jit(solution)/shard_map/gather | solution.py:196
  43.0 2.8 %copy.26 = f32[12,20,20,2]{3,2,1,0:T(8,128)} copy(f32[12,20,20,2]{2,3,1,0:T(2,128)S(1)} %collective-permute-done.4) | data formatting | bytes 76800 | tf_op jit(solution)/shard_map/ppermute | solution.py:27
  46.6 3.7 %copy.27 = f32[12,20,20,2]{3,2,1,0:T(8,128)} copy(f32[12,20,20,2]{2,3,1,0:T(2,128)} %collective-permute-done.5) | data formatting | bytes 76800 | tf_op jit(solution)/shard_map/ppermute | solution.py:29
  50.2 7.0 %pad_maximum_fusion = f32[12,20,20,132]{3,2,1,0:T(8,128)S(1)} fusion(f32[12,20,20,2]{3,2,1,0:T(8,128)} %copy.27, f32[12,20,2,128]{3,2,1,0:T(2,128)S(1)} %collective-permute-done.3, f32[12,2,16,128]{3,2,1,0:T(8,128)S(1)} %copy-done.3, f32[12,16,16,128]{3,2,1,0:T(8,128)S(1)} %constant_dynamic-update-slice_fusion, ...), kind=kLoop, calls=%fused_computation.2 | loop fusion | flops 3801600 | bytes 5068800 | tf_op jit(solution)/shard_map/concatenate | solution.py:25
  57.2 1.8 %slice_bitcast_fusion = (f32[20,20,132]{2,1,0:T(8,128)S(1)}, f32[20,20,132]{2,1,0:T(8,128)S(1)}, f32[20,20,132]{2,1,0:T(8,128)S(1)}, f32[20,20,132]{2,1,0:T(8,12...) fusion(f32[12,20,20,132]{3,2,1,0:T(8,128)S(1)} %pad_maximum_fusion), kind=kLoop, calls=%fused_computation.12 | loop fusion | bytes 5068800 | tf_op jit(solution)/shard_map/squeeze | solution.py:106
  59.0 14.9 %subtract_convert_fusion.1 = (bf16[16,16,128]{2,1,0:T(8,128)(2,1)S(1)}, f32[16,16,128]{2,1,0:T(8,128)S(1)}, f32[16,16,128]{2,1,0:T(8,128)}, f32[16,16,128]{2,1,0...) fusion(f32[16,16]{1,0:T(8,128)S(1)} %get-tuple-element.85, ...), kind=kLoop, calls=%fused_computation.304 | loop fusion | flops 12484608 | bytes 20526080 | tf_op jit(solution)/shard_map/convert.7
  74.0 1.9 %subtract_convert_fusion = bf16[16,16,128]{2,1,0:T(8,128)(2,1)S(1)} fusion(f32[16,16,128]{2,1,0:T(8,128)} %get-tuple-element.26, f32[16,16,128]{2,1,0:T(8,128)} %get-tuple-element.25, f32[16,16,128]{2,1,0:T(8,128)} %get-tuple-element.24, f32[16,16,128]{2,1,0:T(8,128)} %get-tuple-element.23, f32[16,16,128]{2,1,0:T(8,128)} %get-tuple-element.22, ...), kind=kLoop, calls=%fused_computation.303 | loop fusion | flops 2785280 | bytes 1651712 | tf_op jit(solution)/shard_map/convert.6
  77.1 1.1 reshape.879
  78.1 3.4 %fusion.2 = f32[8,64,2]{1,2,0:T(2,128)S(1)} fusion(bf16[8,2,4096]{2,1,0:T(2,128)(2,1)S(1)} %reshape.879, bf16[1,1,8,64,4096]{4,3,2,1,0:T(8,128)(2,1)} %param.10), kind=kOutput, calls=%fused_computation.6 | convolution fusion | flops 8388608 | bytes 4329472 | tf_op jit(solution)/shard_map/bcn,bpn->bpc/dot_general | solution.py:190
  81.6 0.8 fusion.13
  82.4 0.8 fusion.11
  83.2 0.8 fusion.6
  84.1 0.8 fusion.5
  85.0 42.8 %psum.7 = f32[3,2,77]{2,0,1:T(4,128)S(1)} all-reduce(f32[3,2,77]{2,0,1:T(4,128)S(1)} %maximum_multiply_fusion), channel_id=1, replica_groups=mesh['gx'=2,'gy'=4,'gz'=4] {'gx','gy','gz'}, use_global_device_ids=true, to_apply=%region_0.1 | all-reduce | flops 462 | bytes 3696 | tf_op jit(solution)/shard_map/psum | solution.py:197
  (45 shorter events, 4.5 us)
Async XLA Ops:
  0.6 10.2 %copy-start = (f32[6144]{0:T(1024)S(1)}, f32[6144]{0:T(1024)}, u32[]{:S(2)}) copy-start(f32[6144]{0:T(1024)} %param.12) | copy-start | bytes 73732
  0.6 9.4 %copy-start.4 = (s32[1,1,8,64]{3,2,1,0:T(8,128)S(1)}, s32[1,1,8,64]{3,2,1,0:T(8,128)}, u32[]{:S(2)}) copy-start(s32[1,1,8,64]{3,2,1,0:T(8,128)} %param.11) | copy-start | bytes 6148
  3.9 11.3 %collective-permute-start = (f32[12,2,16,128]{3,2,1,0:T(8,128)}, f32[12,2,16,128]{3,2,1,0:T(8,128)S(1)}, u32[]{:S(2)}, u32[]{:S(2)}) collective-permute-start(f32[12,2,16,128]{3,2,1,0:T(8,128)} %get-tuple-element.43), channel_id=1, source_target_pairs={{0,16},{1,17},{2,18},{3,19},{4,20},{5,21},{6,22},{7,23},{8,24},{9,... | collective-permute-start | bytes 589832 | tf_op jit(solution)/shard_map/ppermute | solution.py:27
  8.8 8.5 %collective-permute-start.1 = (f32[12,2,16,128]{3,2,1,0:T(8,128)}, f32[12,2,16,128]{3,2,1,0:T(8,128)S(1)}, u32[]{:S(2)}, u32[]{:S(2)}) collective-permute-start(f32[12,2,16,128]{3,2,1,0:T(8,128)} %get-tuple-element.44), channel_id=1, source_target_pairs={{16,0},{17,1},{18,2},{19,3},{20,4},{21,5},{22,6},{23,7},{24,8},{25... | collective-permute-start | bytes 589832 | tf_op jit(solution)/shard_map/ppermute | solution.py:29
  17.2 1.5 %copy-start.2 = (f32[12,2,16,128]{3,2,1,0:T(8,128)}, f32[12,2,16,128]{3,2,1,0:T(8,128)S(1)}, u32[]{:S(2)}) copy-start(f32[12,2,16,128]{3,2,1,0:T(8,128)S(1)} %collective-permute-done.1) | copy-start | bytes 589828
  17.4 4.2 %collective-permute-start.2 = (f32[12,20,2,128]{3,2,1,0:T(2,128)S(1)}, f32[12,20,2,128]{3,2,1,0:T(2,128)S(1)}, u32[]{:S(2)}, u32[]{:S(2)}) collective-permute-start(f32[12,20,2,128]{3,2,1,0:T(2,128)S(1)} %get-tuple-element.41), channel_id=1, source_target_pairs={{0,4},{4,8},{8,12},{1,5},{5,9},{9,13},{2,6},{6,10},{10,14},{3,7},{... | collective-permute-start | bytes 737288 | tf_op jit(solution)/shard_map/ppermute | solution.py:27
  18.7 5.1 %collective-permute-start.3 = (f32[12,20,2,128]{3,2,1,0:T(2,128)S(1)}, f32[12,20,2,128]{3,2,1,0:T(2,128)S(1)}, u32[]{:S(2)}, u32[]{:S(2)}) collective-permute-start(f32[12,20,2,128]{3,2,1,0:T(2,128)S(1)} %get-tuple-element.42), channel_id=1, source_target_pairs={{4,0},{8,4},{12,8},{5,1},{9,5},{13,9},{6,2},{10,6},{14,10},{7,3},{... | collective-permute-start | bytes 737288 | tf_op jit(solution)/shard_map/ppermute | solution.py:29
  28.8 11.1 %copy-start.1 = (f32[6144]{0:T(1024)S(1)}, f32[6144]{0:T(1024)}, u32[]{:S(2)}) copy-start(f32[6144]{0:T(1024)} %param.13) | copy-start | bytes 73732
  31.8 11.2 %collective-permute-start.4 = (f32[12,20,20,2]{2,3,1,0:T(2,128)S(1)}, f32[12,20,20,2]{2,3,1,0:T(2,128)S(1)}, u32[]{:S(2)}, u32[]{:S(2)}) collective-permute-start(f32[12,20,20,2]{2,3,1,0:T(2,128)S(1)} %copy.32), channel_id=1, source_target_pairs={{0,1},{1,2},{2,3},{4,5},{5,6},{6,7},{8,9},{9,10},{10,11},{12,13},{... | collective-permute-start | bytes 115208 | tf_op jit(solution)/shard_map/ppermute | solution.py:27
  38.4 8.2 %collective-permute-start.5 = (f32[12,20,20,2]{2,3,1,0:T(2,128)S(1)}, f32[12,20,20,2]{2,3,1,0:T(2,128)}, u32[]{:S(2)}, u32[]{:S(2)}) collective-permute-start(f32[12,20,20,2]{2,3,1,0:T(2,128)S(1)} %copy.33), channel_id=1, source_target_pairs={{1,0},{2,1},{3,2},{5,4},{6,5},{7,6},{9,8},{10,9},{11,10},{13,12},{... | collective-permute-start | bytes 115208 | tf_op jit(solution)/shard_map/ppermute | solution.py:29
  43.0 7.2 %copy-start.3 = (f32[12,2,16,128]{3,2,1,0:T(8,128)S(1)}, f32[12,2,16,128]{3,2,1,0:T(8,128)}, u32[]{:S(2)}) copy-start(f32[12,2,16,128]{3,2,1,0:T(8,128)} %copy-done.2) | copy-start | bytes 589828
  77.0 4.6 %copy-start.5 = (f32[77]{0:T(128)S(1)}, f32[77]{0:T(128)}, u32[]{:S(2)}) copy-start(f32[77]{0:T(128)} %constant.112.clone) | copy-start | bytes 928
where the time goes:
time: 130 us; the launch traced here: 129 us
  blocking collectives  42.8 us (33%)
  local copies, waits for them, and re-layouts  30.5 us (23%)
  other arithmetic  27.8 us (21%)
  starting transfers between devices  13.7 us (11%)
  matrix products  8.25 us (6%)
  waiting for transfers between devices  4.98 us (4%)
    psum x1, blocking collectives, shards(): modes = lax.psum(local_modes, ('gx', 'gy', 'gz'))  42.8 us
    another operation x2, other arithmetic  16.9 us
    ppermute x3, starting transfers between devices, padded_2(): lax.ppermute(tail, axis, [(i, (i + 1) % count) for i in range(ends)])  9.67 us
    concatenate x2, other arithmetic, padded_2(): jnp.concatenate([lax.ppermute(tail, axis, [(i, (i + 1) % count) for i in...  8.35 us
    unnamed x16, local copies, waits for them, and re-layouts  7.91 us
    ppermute x3, waiting for transfers between devices, padded_2(): lax.ppermute(head, axis, [((i + 1) % count, i) for i in range(ends)])  4.97 us
    slice x2, local copies, waits for them, and re-layouts, padded_2(): lax.slice_in_dim(cells, cells.shape[dim] - width, cells.shape[dim], axis=...  4.32 us
    ppermute x3, starting transfers between devices, padded_2(): lax.ppermute(head, axis, [((i + 1) % count, i) for i in range(ends)])  4.06 us
  transfers between devices with their start and end apart: 6, of which 3 were waited for; matrix products, arithmetic and copies ran while one was open for 12% of the time, Pallas kernels for 0%

commit v1 on v0

v1 whole, which is shorter than its diff:
```python
import functools
import math

import jax
import jax.numpy as jnp
import numpy as np
from jax import lax
from jax.experimental import pallas as pl
from jax.experimental.pallas import tpu as pltpu
from jax.sharding import PartitionSpec as P

BLK = 16
PTS = 2048
SPHERES = 3
LMAX = 8
AXES = ("gx", "gy", "gz")
MODES = (LMAX + 1) ** 2 - 4
ROWS = 24
NEAR = 1.0 / 3.0
FAR = 1.0 / 24.0
XX, XY, XZ, YY, YZ, ZZ = range(6)
VMEM = pltpu.VMEM
LIMIT = 24 * 1024 * 1024


def recurrence():
    table = np.zeros((ROWS, 128), np.float32)
    norm = lambda degree: math.sqrt((2 * degree + 1) / (4.0 * math.pi))
    for order in range(-LMAX, LMAX + 1):
        low = max(2, abs(order))
        row = order + LMAX
        gap = lambda degree: math.sqrt((degree**2 - order**2) * (degree**2 - 4))
        for degree in range(low, LMAX):
            base = 3 * (degree - 2)
            lift = degree * gap(degree + 1)
            scale = norm(degree + 1) / norm(degree) * (2 * degree + 1) / lift
            table[row, base] = scale * degree * (degree + 1)
            table[row, base + 1] = -scale * 2 * order
            if degree > low:
                table[row, base + 2] = norm(degree + 1) / norm(degree - 1) * (degree + 1) * gap(degree) / lift
        step = min(max(order, -2), 2) + 2 if low == 2 else (low + 2 if order > 0 else 0)
        lower = step - 2 - order
        lead = (-1.0) ** order * math.sqrt(
            math.factorial(low + order)
            * math.factorial(low - order)
            * (2 * low + 1)
            / (4.0 * math.pi * math.factorial(low - 2) * math.factorial(low + 2))
        )
        table[row, 127] = lead * math.comb(low + 2, step) * math.comb(low - 2, lower) * (-1.0) ** (low - step + 2)
    return table


def frame(x, y, z):
    rho2 = x * x + y * y
    inv_rho = lax.rsqrt(rho2)
    inv_r = lax.rsqrt(rho2 + z * z)
    cos_p = x * inv_rho
    sin_p = y * inv_rho
    cos_t = z * inv_r
    sin_t = rho2 * inv_rho * inv_r
    cc = cos_p * cos_p
    ss = sin_p * sin_p
    tt = cos_t * cos_t
    cs = cos_p * sin_p
    st = sin_t * cos_t
    twice_p = (tt * cc - ss, cs * (tt + 1.0), -(st * cos_p), tt * ss - cc, -(st * sin_p), sin_t * sin_t)
    q_diag = cos_t * cs
    twice_q = (cos_t * (cc - ss), sin_t * sin_p, -(sin_t * cos_p))
    return twice_p, q_diag, twice_q


def total(terms):
    terms = [term for term in terms if term is not None]
    return functools.reduce(lambda one, two: one + two, terms)


def times(one, two):
    return None if one is None or two is None else one * two


def minus(one, two):
    if two is None:
        return one
    return -two if one is None else one - two


def contract(geometry, electric, magnetic):
    twice_p, q_diag, twice_q = geometry
    e, b = electric, magnetic
    half = total([times(twice_p[i], e[i]) for i in (XX, YY, ZZ)]) * 0.5
    real_e = half + total([times(twice_p[i], e[i]) for i in (XY, XZ, YZ)])
    off = (XY, XZ, YZ)
    imag_e = q_diag * (e[YY] - e[XX]) + total([twice_q[n] * e[i] for n, i in enumerate(off)])
    real_b = total([times(2.0 * q_diag, minus(b[YY], b[XX]))] + [times(twice_q[n], b[i]) for n, i in enumerate(off)])
    imag_b = total([times(twice_p[i], b[i]) for i in range(6)])
    return real_e - real_b, -(imag_e + imag_b)


def curl_part(axis, d):
    yz, xz, xy, diff = d
    if axis == 0:
        return [None, -xz, xy, -yz, diff, yz]
    if axis == 1:
        return [xz, yz, diff, None, -xy, -xz]
    return [-xy, diff, -yz, xy, xz, None]


DIFFS = ((YY, ZZ), (ZZ, XX), (XX, YY))


def iota(shape, dim):
    return lax.broadcasted_iota(jnp.int32, shape, dim)


def origin(axis, cells):
    place = lax.axis_index(axis)
    count = lax.axis_size(axis)
    return (place * cells).astype(jnp.float32) + (0.5 - count * cells / 2.0), place


def face_part(axis, near, far, sign, geometry):
    h_near, k_near = near if near is not None else (None, None)
    h_far, k_far = far
    if near is None:
        e = [h * FAR for h in h_far]
        d = [k * (-FAR * sign) for k in k_far]
    else:
        e = [f * FAR - n * (2.0 / 3.0) for n, f in zip(h_near, h_far)]
        d = [(n * NEAR - f * FAR) * sign for n, f in zip(k_near, k_far)]
    return contract(geometry, e, curl_part(axis, d))


def pick_k(axis, load):
    one, two = DIFFS[axis]
    return [load(6 + YZ), load(6 + XZ), load(6 + XY), load(6 + one) - load(6 + two)]


def faces_kernel(slots, metric, curvature, *refs):
    nx = slots[0]
    ny = slots[1]
    x_out = refs[:nx]
    y_out = refs[nx : nx + ny]
    z_out, z_fix, fields, sems = refs[nx + ny :]
    copies = []
    for comp in range(6):
        for base, source in ((0, metric), (6, curvature)):
            copies.append(
                pltpu.make_async_copy(
                    source.at[comp],
                    fields.at[base + comp, pl.ds(2, BLK), pl.ds(8, BLK), :],
                    sems.at[base + comp],
                )
            )
    for copy in copies:
        copy.start()
    blank = jnp.zeros((12, BLK, 8, 128), jnp.float32)
    fields[:, pl.ds(2, BLK), pl.ds(0, 8), :] = blank
    fields[:, pl.ds(2, BLK), pl.ds(24, 8), :] = blank
    plane = jnp.zeros((12, 2, BLK, 128), jnp.float32)
    fields[:, pl.ds(0, 2), pl.ds(8, BLK), :] = plane
    fields[:, pl.ds(BLK + 2, 2), pl.ds(8, BLK), :] = plane
    for copy in copies:
        copy.wait()
    x0, ix = origin("gx", BLK)
    y0, iy = origin("gy", BLK)
    z0, iz = origin("gz", 128)
    slab = (BLK, 128)
    rows = iota(slab, 0).astype(jnp.float32)
    lanes = iota(slab, 1).astype(jnp.float32)
    z = lanes + z0
    for slot in range(nx):
        high = (ix % 2) == slot
        near_at = jnp.where(high, BLK + 1, 2)
        far_at = jnp.where(high, BLK, 3)
        sign = jnp.where(high, -1.0, 1.0)
        near = [fields[c, near_at, pl.ds(8, BLK), :] for c in range(6)]
        far = [fields[c, far_at, pl.ds(8, BLK), :] for c in range(6)]
        k_near = pick_k(0, lambda c: fields[c, near_at, pl.ds(8, BLK), :])
        k_far = pick_k(0, lambda c: fields[c, far_at, pl.ds(8, BLK), :])
        y = rows + y0
        for layer in range(2):
            x = jnp.where(high, x0 + (BLK + layer), x0 - (1 + layer))
            geometry = frame(x, y, z)
            if layer == 0:
                real, imag = face_part(0, (near, k_near), (far, k_far), sign, geometry)
            else:
                real, imag = face_part(0, None, (near, k_near), sign, geometry)
            x_out[slot][0, layer] = real
            x_out[slot][1, layer] = imag
    for slot in range(ny):
        high = (iy % 2) == slot
        near_at = jnp.where(high, 8 + BLK - 1, 8)
        far_at = jnp.where(high, 8 + BLK - 2, 9)
        sign = jnp.where(high, -1.0, 1.0)

        def line(c, at):
            return fields.reshape(12 * 20 * 32, 128)[pl.ds(c * 640 + 64 + at, BLK, stride=32), :]

        near = [line(c, near_at) for c in range(6)]
        far = [line(c, far_at) for c in range(6)]
        k_near = pick_k(1, lambda c: line(c, near_at))
        k_far = pick_k(1, lambda c: line(c, far_at))
        x = rows + x0
        for layer in range(2):
            y = jnp.where(high, y0 + (BLK + layer), y0 - (1 + layer))
            geometry = frame(x, y, z)
            if layer == 0:
                real, imag = face_part(1, (near, k_near), (far, k_far), sign, geometry)
            else:
                real, imag = face_part(1, None, (near, k_near), sign, geometry)
            y_out[slot][0, layer] = real
            y_out[slot][1, layer] = imag
    lane = iota((8, 128), 1)
    group = lane // 4

    def packed(load):
        out = jnp.zeros((8, 128), jnp.float32)
        for j in range(32):
            value = load(j // 2, j % 2)
            out = jnp.where(group == j, pltpu.roll(value, (2 + 4 * j) % 128, 1), out)
        return out

    def piece(c):
        return lambda x, half: fields[c, 2 + x, pl.ds(8 + 8 * half, 8), :]

    h_all = [packed(piece(c)) for c in range(6)]
    one, two = DIFFS[2]
    k_all = [packed(piece(6 + c)) for c in (YZ, XZ, XY)]
    k_all.append(packed(lambda x, half: piece(6 + one)(x, half) - piece(6 + two)(x, half)))
    q = lane % 4
    upper = q >= 2
    inner = (q == 1) | (q == 2)

    def shifted(value, by):
        return jnp.where(upper, pltpu.roll(value, by, 1), pltpu.roll(value, 128 - by, 1))

    e = [shifted(h, 2) * FAR - jnp.where(inner, shifted(h, 1), 0.0) * (2.0 / 3.0) for h in h_all]
    sign = jnp.where(upper, -1.0, 1.0)
    d = [(jnp.where(inner, shifted(k, 1), 0.0) * NEAR - shifted(k, 2) * FAR) * sign for k in k_all]
    magnetic = curl_part(2, d)
    x = (lane // 8).astype(jnp.float32) + x0
    y = (iota((8, 128), 0) + 8 * (group % 2)).astype(jnp.float32) + y0
    z_here = jnp.where(upper, q - 2, q + 126).astype(jnp.float32) + z0
    z_there = z_here + jnp.where(upper, 128.0, -128.0)
    for out, z_at in ((z_out, z_there), (z_fix, z_here)):
        real, imag = contract(frame(x, y, z_at), e, magnetic)
        out[0] = real
        out[1] = imag


def sin_cos(x):
    x2 = x * x
    sine = 0.0
    cosine = 0.0
    for n in range(6, -1, -1):
        sine = sine * x2 + (-1.0) ** n / math.factorial(2 * n + 1)
    for n in range(7, -1, -1):
        cosine = cosine * x2 + (-1.0) ** n / math.factorial(2 * n)
    return sine * x, cosine


def split3(value):
    one = value.astype(jnp.bfloat16)
    rest = value - one.astype(jnp.float32)
    two = rest.astype(jnp.bfloat16)
    three = (rest - two.astype(jnp.float32)).astype(jnp.bfloat16)
    return one, two, three


def interior_kernel(fields, ids_far, theta_far, phi_far, coefs_far, weights, local, harm, ids, loaded, *scratch):
    lists, theta, phi, coefs, sems = scratch
    small = [
        pltpu.make_async_copy(source, target, sems.at[n])
        for n, (source, target) in enumerate(
            ((ids_far, lists), (theta_far, theta), (phi_far, phi), (coefs_far, coefs))
        )
    ]
    copy = pltpu.make_async_copy(weights, loaded, sems.at[4])
    for each in small:
        each.start()
    copy.start()
    x0, _ = origin("gx", BLK)
    y0, _ = origin("gy", BLK)
    z0, _ = origin("gz", 128)
    slab = (BLK, 128)
    y = iota(slab, 0).astype(jnp.float32) + y0
    z = iota(slab, 1).astype(jnp.float32) + z0

    def plane(i, carry):
        def at(c, dx=0, dy=0):
            return fields[c, i + (2 + dx), pl.ds(8 + dy, BLK), :]

        def roll(value, by):
            return pltpu.roll(value, by % 128, 1)

        geometry = frame(x0 + i.astype(jnp.float32), y, z)
        k = [at(6 + c) for c in range(6)]
        trace = k[XX] + k[YY] + k[ZZ]
        prod = {}

        def mul(a, b):
            key = (min(a, b), max(a, b))
            if key not in prod:
                prod[key] = k[key[0]] * k[key[1]]
            return prod[key]

        pairs = ((XX, XY, XZ), (XY, YY, YZ), (XZ, YZ, ZZ))
        e = []
        for row in range(3):
            for col in range(row, 3):
                c = pairs[row][col]
                h = at(c)
                one = (at(c, -1) + at(c, 1)) + (at(c, 0, -1) + at(c, 0, 1)) + (roll(h, 1) + roll(h, -1))
                two = (at(c, -2) + at(c, 2)) + (at(c, 0, -2) + at(c, 0, 2)) + (roll(h, 2) + roll(h, -2))
                square = total([mul(pairs[row][n], pairs[n][col]) for n in range(3)])
                e.append(two * FAR - one * (2.0 / 3.0) + h * 3.75 + (trace * k[c] - square))

        def slope(m2, m1, p1, p2):
            return (p1 - m1) * NEAR - (p2 - m2) * FAR

        steps = (-2, -1, 1, 2)
        along_x = [pick_k(0, lambda c, s=s: at(c, s)) for s in steps]
        dx = [slope(*[along_x[n][f] for n in range(4)]) for f in range(4)]
        along_y = [pick_k(1, lambda c, s=s: at(c, 0, s)) for s in steps]
        dy = [slope(*[along_y[n][f] for n in range(4)]) for f in range(4)]
        here = [k[YZ], k[XZ], k[XY], k[XX] - k[YY]]
        dz = [slope(*[roll(f, -s) for s in steps]) for f in here]
        parts = [curl_part(axis, d) for axis, d in enumerate((dx, dy, dz))]
        magnetic = [total([part[c] for part in parts]) for c in range(6)]
        real, imag = contract(geometry, e, magnetic)
        local[0, i] = real
        local[1, i] = imag
        return carry

    lax.fori_loop(0, BLK, plane, 0)
    for each in small:
        each.wait()
    count = ids.shape[1]
    id_row = jnp.concatenate([lists[n : n + 1] for n in range(lists.shape[0])], axis=1)
    ids[...] = id_row
    wide = (theta.shape[0], count)
    pick = jnp.where(iota(wide, 0) == id_row // 128, 1.0, 0.0).astype(jnp.bfloat16)
    tables = jnp.concatenate([theta[...], phi[...]], axis=1)
    left = jnp.concatenate(split3(tables), axis=0)
    right = jnp.concatenate([pick] * 3, axis=0)
    found = lax.dot_general(left, right, (((0,), (0,)), ((), ())), preferred_element_type=jnp.float32)
    mine = iota((128, count), 0) == id_row % 128
    half_t = jnp.sum(jnp.where(mine, found[:128], 0.0), axis=0, keepdims=True) * 0.5
    half_p = jnp.sum(jnp.where(mine, found[128:], 0.0), axis=0, keepdims=True) * 0.5
    sines, cosines = sin_cos(jnp.concatenate([half_t, half_p, jnp.zeros((6, count), jnp.float32)], axis=0))
    sin_h, cos_h = sines[0:1], cosines[0:1]
    cos_t = cos_h * cos_h - sin_h * sin_h
    sin_p = 2.0 * sines[1:2] * cosines[1:2]
    cos_p = 1.0 - 2.0 * sines[1:2] * sines[1:2]
    shape = (ROWS, count)
    order = iota(shape, 0) - LMAX
    size = jnp.abs(order)
    lowest = jnp.maximum(size, 2)
    tilt = jnp.clip(order, -2, 2)
    unit_r = jnp.ones(shape, jnp.float32)
    unit_i = jnp.zeros(shape, jnp.float32)
    start = jnp.where(size <= LMAX, coefs[:, 127:128], 0.0)
    step_r, step_i, step_c, step_s = cos_p, sin_p, cos_h, sin_h
    for bit in range(4):
        has = (size >> bit) & 1 == 1
        new_r = unit_r * step_r - unit_i * step_i
        new_i = unit_r * step_i + unit_i * step_r
        unit_r = jnp.where(has, new_r, unit_r)
        unit_i = jnp.where(has, new_i, unit_i)
        start = jnp.where(((lowest + tilt) >> bit) & 1 == 1, start * step_c, start)
        start = jnp.where(((lowest - tilt) >> bit) & 1 == 1, start * step_s, start)
        step_r, step_i = step_r * step_r - step_i * step_i, 2.0 * step_r * step_i
        step_c = step_c * step_c
        step_s = step_s * step_s
    unit_i = jnp.where(order < 0, -unit_i, unit_i)
    before = jnp.zeros(shape, jnp.float32)
    now = jnp.where(lowest == 2, start, 0.0)
    for degree in range(2, LMAX + 1):
        if degree > 2:
            base = 3 * (degree - 3)
            slope = coefs[:, base : base + 1] * cos_t + coefs[:, base + 1 : base + 2]
            after = slope * now - coefs[:, base + 2 : base + 3] * before
            before, now = now, jnp.where(lowest == degree, start, after)
        at = degree * degree - 4
        width = 2 * degree + 1
        low = LMAX - degree
        harm[pl.ds(at, width), pl.ds(0, count)] = (now * unit_r)[low : low + width]
        harm[pl.ds(at, width), pl.ds(count, count)] = (now * unit_i)[low : low + width]
    harm[pl.ds(MODES, 80 - MODES), :] = jnp.zeros((80 - MODES, 2 * count), jnp.float32)
    copy.wait()


def finish_kernel(slots, local, *refs):
    nx, ny, nz = slots
    x_in = refs[:nx]
    y_in = refs[nx : nx + ny]
    z_in = refs[nx + ny : nx + ny + nz]
    z_fix, weights, harm, ids, psi, modes, work, stored, flat, sem = refs[nx + ny + nz :]
    ix = lax.axis_index("gx")
    iy = lax.axis_index("gy")
    iz = lax.axis_index("gz")
    lane = iota((8, 128), 1)
    q = lane % 4
    edge = (lane >= 126) | (lane < 2)
    for part in range(2):
        got = [ref[part] for ref in z_in]
        if nz == 1:
            got = got * 2
        even = (iz % 2) == 0
        plus = jnp.where(even, got[0], got[1])
        less = jnp.where(even, got[1], got[0])
        z_part = jnp.where(q < 2, plus, less)
        if nz == 1:
            z_part = jnp.where((q < 2) == even, got[0], 0.0)
        z_part = z_part - z_fix[part]
        for j in range(32):
            moved = pltpu.roll(z_part, (126 - 4 * j) % 128, 1)
            value = local[part, j // 2, pl.ds(8 * (j % 2), 8), :]
            work[part, pl.ds(8 * j, 8), :] = value + jnp.where(edge, moved, 0.0)
    for part in range(2):
        for slot in range(nx):
            high = (ix % 2) == slot
            for layer in range(2):
                at = jnp.where(high, BLK - 1 - layer, layer) * BLK
                span = pl.ds(pl.multiple_of(at, BLK), BLK)
                work[part, span, :] = work[part, span, :] + x_in[slot][part, layer]
        for slot in range(ny):
            high = (iy % 2) == slot
            for layer in range(2):
                at = jnp.where(high, BLK - 1 - layer, layer)
                span = pl.ds(part * 256 + at, BLK, stride=BLK)
                both = work.reshape(512, 128)
                both[span, :] = both[span, :] + y_in[slot][part, layer]
    row = iota((8, 128), 0)
    source = (lane // BLK + row + 1) % 8
    for part in range(2):
        for x in range(BLK):
            rounded = work[part, pl.ds(BLK * x, BLK), :].astype(jnp.bfloat16)
            stored[part, x] = rounded
            values = rounded.astype(jnp.float32)
            for half in range(2):
                value = values[8 * half : 8 * half + 8]
                value = pltpu.roll(value, 0, 1, stride=BLK, stride_axis=0)
                value = jnp.take_along_axis(value, source, axis=0)
                value = pltpu.roll(value, BLK, 1, stride=BLK, stride_axis=0)
                flat[pl.ds(8 * part, 8), pl.ds((2 * x + half) * 128, 128)] = value
    copy = pltpu.make_async_copy(stored, psi, sem)
    copy.start()
    count = ids.shape[1]
    blocks = flat[...].astype(jnp.bfloat16)
    product = lax.dot_general(
        blocks, weights[...], (((1,), (1,)), ((), ())), preferred_element_type=jnp.float32
    )
    own = iota((8, count), 0) == 7 - iota((8, count), 1) // (count // 8)
    real = jnp.sum(jnp.where(own, product[:8], 0.0), axis=0, keepdims=True)
    imag = jnp.sum(jnp.where(own, product[8:], 0.0), axis=0, keepdims=True)
    row = iota((8, count), 0)
    live = ids[...] // PTS == row // 2
    first = row % 2 == 0
    left = jnp.where(live, jnp.where(first, real, imag), 0.0)
    right = jnp.where(live, jnp.where(first, imag, -real), 0.0)
    sums = lax.dot_general(
        jnp.concatenate([left, right], axis=1),
        harm[...],
        (((1,), (1,)), ((), ())),
        precision=lax.Precision.HIGHEST,
        preferred_element_type=jnp.float32,
    )
    sums = sums * (4.0 * math.pi / PTS)
    sums = jnp.concatenate([sums, jnp.zeros((8, 128 - 80), jnp.float32)], axis=1)
    modes[...] = jnp.broadcast_to(sums[None], modes.shape)
    copy.wait()


def matching(axis, slot):
    perm = []
    for low in range(slot, lax.axis_size(axis) - 1, 2):
        perm += [(low, low + 1), (low + 1, low)]
    return perm


def shards(metric_pert, curvature, interp_weights, point_ids, theta, phi):
    f32 = jnp.float32
    hbm = pl.BlockSpec(memory_space=pltpu.HBM)
    far = lambda value: pltpu.with_memory_space_constraint(value, pltpu.HBM)
    close = lambda value: pltpu.with_memory_space_constraint(value, VMEM)
    vmem = pl.BlockSpec(memory_space=VMEM)
    slots = tuple(min(2, lax.axis_size(axis) - 1) for axis in AXES)
    nx, ny, nz = slots
    count = point_ids.size
    lists = point_ids.shape[2:]
    cells = BLK * BLK * BLK
    face = VMEM((2, 2, BLK, 128), f32)
    edge = VMEM((2, 8, 128), f32)
    params = pltpu.CompilerParams(vmem_limit_bytes=LIMIT)
    first = pl.pallas_call(
        functools.partial(faces_kernel, slots),
        out_shape=[face] * (nx + ny) + [edge, edge, VMEM((12, 20, 32, 128), f32)],
        in_specs=[hbm] * 2,
        out_specs=[vmem] * (nx + ny + 3),
        scratch_shapes=[pltpu.SemaphoreType.DMA((12,))],
        compiler_params=params,
        name="faces",
    )(far(metric_pert), far(curvature))
    x_send, y_send = first[:nx], first[nx : nx + ny]
    z_send, z_fix, fields = first[nx + ny :]
    x_got = [lax.ppermute(x_send[slot], "gx", matching("gx", slot)) for slot in range(nx)]
    y_got = [lax.ppermute(y_send[slot], "gy", matching("gy", slot)) for slot in range(ny)]
    z_got = [lax.ppermute(z_send, "gz", matching("gz", slot)) for slot in range(nz)]
    weights = interp_weights.reshape(count, cells)
    local, harm, ids, loaded = pl.pallas_call(
        interior_kernel,
        out_shape=[VMEM((2, BLK, BLK, 128), f32), VMEM((80, 2 * count), f32), VMEM((1, count), jnp.int32), VMEM((count, cells), jnp.bfloat16)],
        in_specs=[vmem] + [hbm] * 5,
        out_specs=[vmem] * 4,
        scratch_shapes=[
            VMEM(lists, jnp.int32),
            VMEM((theta.size // 128, 128), f32),
            VMEM((theta.size // 128, 128), f32),
            VMEM((ROWS, 128), f32),
            pltpu.SemaphoreType.DMA((5,)),
        ],
        compiler_params=params,
        cost_estimate=pl.CostEstimate(flops=20_000_000, bytes_accessed=8_000_000, transcendentals=0),
        name="interior",
    )(
        close(fields),
        far(point_ids.reshape(lists)),
        far(theta.reshape(-1, 128)),
        far(phi.reshape(-1, 128)),
        far(jnp.asarray(recurrence())),
        far(weights),
    )
    total_devices = math.prod(lax.axis_size(axis) for axis in AXES)
    psi, modes = pl.pallas_call(
        functools.partial(finish_kernel, slots),
        out_shape=[pltpu.HBM((2, BLK, BLK, 128), jnp.bfloat16), VMEM((total_devices, 8, 128), f32)],
        in_specs=[vmem] * (1 + nx + ny + nz + 4),
        out_specs=[hbm, vmem],
        scratch_shapes=[
            VMEM((2, 256, 128), f32),
            VMEM((2, BLK, BLK, 128), jnp.bfloat16),
            VMEM((16, cells), f32),
            pltpu.SemaphoreType.DMA,
        ],
        compiler_params=params,
        name="finish",
    )(*map(close, (local, *x_got, *y_got, *z_got, z_fix, loaded, harm, ids)))
    modes = lax.all_to_all(modes, AXES, 0, 0, tiled=True).sum(0)
    return psi, modes[: 2 * SPHERES, :MODES].reshape(SPHERES, 2, MODES)


def solution(mesh):
    in_specs = (
        P(None, "gx", "gy", "gz"),
        P(None, "gx", "gy", "gz"),
        P("gx", "gy", "gz", None, None),
        P("gx", "gy", "gz", None),
        P(),
        P(),
    )
    out_specs = (P(None, "gx", "gy", "gz"), P())
    return jax.shard_map(shards, mesh=mesh, in_specs=in_specs, out_specs=out_specs, check_vma=False)
```

time: 130 us -> 31.8 us (0.24)
  local copies, waits for them, and re-layouts: 30.5 us -> 0.59 us
  other arithmetic: 27.8 us -> 0.04 us
  blocking collectives: 42.8 us -> 15.8 us
  Pallas kernels: 0 us -> 8.51 us
  matrix products: 8.25 us -> 0 us
  starting transfers between devices: 13.7 us -> 5.98 us
  waiting for transfers between devices: 4.98 us -> 0.01 us
    psum x1 -> x0, blocking collectives: 42.8 us -> none  [shards(): modes = lax.psum(local_modes, ('gx', 'gy', 'gz'))]
    another operation x3 -> x0, other arithmetic: 17.5 us -> none
    all_to_all x0 -> x1, blocking collectives: none -> 15.8 us  [shards(): modes = lax.all_to_all(modes, AXES, 0, 0, tiled=True).sum(0)]
    pallas_call x0 -> x3, Pallas kernels: none -> 8.51 us  [the longest x1 3.35 us: shards(): pl.pallas_call(interior_kernel, out_shape=[VMEM((2, BLK, BLK, 128), f32),...]
    concatenate x2 -> x0, other arithmetic: 8.35 us -> none  [padded_2(): jnp.concatenate([lax.ppermute(tail, axis, [(i, (i + 1) % count) for i in...]
    dot_general x6 -> x0, matrix products: 8.25 us -> none  [the longest x1 3.37 us: shards(): jnp.einsum('bcn,bpn->bpc', blocks, weights, preferred_element_type=jnp.fl...]
    unnamed x16 -> x0, local copies, waits for them, and re-layouts: 7.91 us -> none
    ppermute x6 -> x5, starting transfers between devices: 13.7 us -> 5.98 us  [the longest x1 3.03 us: shards(): lax.ppermute(x_send[slot], 'gx', matching('gx', slot))]
  transfers between devices with their start and end apart: 6 -> 5, of which waited for: 3 -> 0; matrix products, arithmetic and copies ran while one was open for 12% -> 0% of each run, Pallas kernels for 0% -> 11%
where the time goes in v1:
time: 31.8 us; the launch traced here: 31.6 us
  blocking collectives  15.8 us (50%)
  Pallas kernels  8.51 us (27%)
  starting transfers between devices  5.98 us (19%)
  between operations  0.71 us (2%)
  local copies, waits for them, and re-layouts  0.59 us (2%)
    all_to_all x1, blocking collectives, shards(): modes = lax.all_to_all(modes, AXES, 0, 0, tiled=True).sum(0)  15.8 us
    pallas_call x1, Pallas kernels, shards(): pl.pallas_call(interior_kernel, out_shape=[VMEM((2, BLK, BLK, 128), f32),...  3.35 us
    ppermute x1, starting transfers between devices, shards(): lax.ppermute(x_send[slot], 'gx', matching('gx', slot))  3.03 us
    pallas_call x1, Pallas kernels, shards(): pl.pallas_call(functools.partial(finish_kernel, slots), out_shape=[pltpu....  2.66 us
    pallas_call x1, Pallas kernels, shards(): pl.pallas_call(functools.partial(faces_kernel, slots), out_shape=[face] *...  2.5 us
    ppermute x2, starting transfers between devices, shards(): lax.ppermute(z_send, 'gz', matching('gz', slot))  2.29 us
    ppermute x2, starting transfers between devices, shards(): lax.ppermute(y_send[slot], 'gy', matching('gy', slot))  0.65 us
  transfers between devices with their start and end apart: 5, of which 0 were waited for; matrix products, arithmetic and copies ran while one was open for 0% of the time, Pallas kernels for 11%

profile of v1, /device:TPU:0, one launch (start us, length us, event | category | flops | bytes accessed | tf_op | source)
XLA Modules:
  0.0 31.6 jit_solution(15420487549484459628)
XLA Ops:
  0.6 2.5 %faces.1 = (f32[2,2,16,128]{3,2,1,0:T(8,128)S(1)}, f32[2,2,16,128]{3,2,1,0:T(8,128)S(1)}, f32[2,2,16,128]{3,2,1,0:T(8,128)S(1)}, f32[2,8,128]{2,1,0:T(8,128)S(1)...) custom-call(f32[6,16,16,128]{3,2,1,0:T(8,128)} %metric.1, f32[6,16,16,128]{3,2,1,0:T(8,128)} %curvature.1), custom_call_target="tpu_custom_call" | custom-call | tf_op jit(solution)/shard_map/faces/pallas_call | solution.py:496
  3.1 3.0 %collective-permute-start = (f32[2,2,16,128]{3,2,1,0:T(8,128)S(1)}, f32[2,2,16,128]{3,2,1,0:T(8,128)S(1)}, u32[]{:S(2)}, u32[]{:S(2)}) collective-permute-start(f32[2,2,16,128]{3,2,1,0:T(8,128)S(1)} %get-tuple-element.16), channel_id=1, source_target_pairs={{0,16},{16,0},{1,17},{17,1},{2,18},{18,2},{3,19},{19,3},{4,20},{20... | collective-permute-start | bytes 98312 | tf_op jit(solution)/shard_map/ppermute | solution.py:507
  6.2 0.0 collective-permute-start.1
  6.2 0.7 %collective-permute-start.2 = (f32[2,2,16,128]{3,2,1,0:T(8,128)S(1)}, f32[2,2,16,128]{3,2,1,0:T(8,128)S(1)}, u32[]{:S(2)}, u32[]{:S(2)}) collective-permute-start(f32[2,2,16,128]{3,2,1,0:T(8,128)S(1)} %get-tuple-element.18), channel_id=1, source_target_pairs={{4,8},{8,4},{5,9},{9,5},{6,10},{10,6},{7,11},{11,7},{20,24},{24,20... | collective-permute-start | bytes 98312 | tf_op jit(solution)/shard_map/ppermute | solution.py:508
  6.8 1.6 %collective-permute-start.3 = (f32[2,8,128]{2,1,0:T(8,128)S(1)}, f32[2,8,128]{2,1,0:T(8,128)S(1)}, u32[]{:S(2)}, u32[]{:S(2)}) collective-permute-start(f32[2,8,128]{2,1,0:T(8,128)S(1)} %get-tuple-element.19), channel_id=1, source_target_pairs={{0,1},{1,0},{2,3},{3,2},{4,5},{5,4},{6,7},{7,6},{8,9},{9,8},{10,11... | collective-permute-start | bytes 24584 | tf_op jit(solution)/shard_map/ppermute | solution.py:509
  8.5 0.6 %collective-permute-start.4 = (f32[2,8,128]{2,1,0:T(8,128)S(1)}, f32[2,8,128]{2,1,0:T(8,128)S(1)}, u32[]{:S(2)}, u32[]{:S(2)}) collective-permute-start(f32[2,8,128]{2,1,0:T(8,128)S(1)} %get-tuple-element.19), channel_id=1, source_target_pairs={{1,2},{2,1},{5,6},{6,5},{9,10},{10,9},{13,14},{14,13},{17,18},{18,... | collective-permute-start | bytes 24584 | tf_op jit(solution)/shard_map/ppermute | solution.py:509
  9.1 3.4 %interior.1 = (f32[2,16,16,128]{3,2,1,0:T(8,128)S(1)}, f32[80,1024]{1,0:T(8,128)S(1)}, s32[1,512]{1,0:T(1,128)S(1)}, bf16[512,4096]{1,0:T(8,128)(2,1)S(1)}) custom-call(f32[12,20,32,128]{3,2,1,0:T(8,128)S(1)} %get-tuple-element.14.fields, s32[8,64]{1,0:T(8,128)} %bitcast.9, f32[48,128]{1,0:T(8,128)} %bitcast.6, f32[48,128]{1,0:T(8,128)} %bitcast.7, ...), custom_call_target="tpu_custom_call" | custom-call | flops 20000000 | bytes 8000000 | tf_op jit(solution)/shard_map/interior/pallas_call | solution.py:511
  12.5 0.0 collective-permute-done.3.refs_3_
  12.5 0.0 collective-permute-done.4.refs_4_
  12.5 0.0 collective-permute-done.refs_0_
  12.5 0.0 collective-permute-done.1.refs_1_
  12.5 0.0 collective-permute-done.2.refs_2_
  12.5 2.7 %finish.1 = (bf16[2,16,16,128]{3,2,1,0:T(8,128)(2,1)}, f32[32,8,128]{2,1,0:T(8,128)S(1)}) custom-call(f32[2,16,16,128]{3,2,1,0:T(8,128)S(1)} %get-tuple-element.15.local, f32[2,2,16,128]{3,2,1,0:T(8,128)S(1)} %collective-permute-done.refs_0_, f32[2,2,16,128]{3,2,1,0:T(8,128)S(1)} %collective-permute-done.1.refs_1_, ...), custom_call_target="tpu_custom_call" | custom-call | tf_op jit(solution)/shard_map/finish/pallas_call | solution.py:535
  15.2 15.8 %all_to_all.5 = f32[32,8,128]{2,1,0:T(8,128)S(1)} all-to-all(f32[32,8,128]{2,1,0:T(8,128)S(1)} %get-tuple-element.25), channel_id=1, replica_groups=mesh['gx'=2,'gy'=4,'gz'=4] {'gx','gy','gz'}, dimensions={0} | all-to-all | bytes 262144 | tf_op jit(solution)/shard_map/all_to_all | solution.py:549
  31.0 0.6 %reshape.23 = f32[3,2,77]{2,1,0:T(2,128)} reshape(f32[6,77]{1,0:T(8,128)S(1)} %bitcast.8) | data formatting | bytes 3696 | tf_op jit(solution)/shard_map/reshape | solution.py:550
  (1 shorter events, 0.0 us)
Async XLA Ops:
  3.1 9.4 %collective-permute-start = (f32[2,2,16,128]{3,2,1,0:T(8,128)S(1)}, f32[2,2,16,128]{3,2,1,0:T(8,128)S(1)}, u32[]{:S(2)}, u32[]{:S(2)}) collective-permute-start(f32[2,2,16,128]{3,2,1,0:T(8,128)S(1)} %get-tuple-element.16), channel_id=1, source_target_pairs={{0,16},{16,0},{1,17},{17,1},{2,18},{18,2},{3,19},{19,3},{4,20},{20... | collective-permute-start | bytes 98312 | tf_op jit(solution)/shard_map/ppermute | solution.py:507
  6.2 6.4 %collective-permute-start.1 = (f32[2,2,16,128]{3,2,1,0:T(8,128)S(1)}, f32[2,2,16,128]{3,2,1,0:T(8,128)S(1)}, u32[]{:S(2)}, u32[]{:S(2)}) collective-permute-start(f32[2,2,16,128]{3,2,1,0:T(8,128)S(1)} %get-tuple-element.17), channel_id=1, source_target_pairs={{0,4},{4,0},{8,12},{12,8},{1,5},{5,1},{9,13},{13,9},{2,6},{6,2},{1... | collective-permute-start | bytes 98312 | tf_op jit(solution)/shard_map/ppermute | solution.py:508
  6.2 6.4 %collective-permute-start.2 = (f32[2,2,16,128]{3,2,1,0:T(8,128)S(1)}, f32[2,2,16,128]{3,2,1,0:T(8,128)S(1)}, u32[]{:S(2)}, u32[]{:S(2)}) collective-permute-start(f32[2,2,16,128]{3,2,1,0:T(8,128)S(1)} %get-tuple-element.18), channel_id=1, source_target_pairs={{4,8},{8,4},{5,9},{9,5},{6,10},{10,6},{7,11},{11,7},{20,24},{24,20... | collective-permute-start | bytes 98312 | tf_op jit(solution)/shard_map/ppermute | solution.py:508
  6.8 5.7 %collective-permute-start.3 = (f32[2,8,128]{2,1,0:T(8,128)S(1)}, f32[2,8,128]{2,1,0:T(8,128)S(1)}, u32[]{:S(2)}, u32[]{:S(2)}) collective-permute-start(f32[2,8,128]{2,1,0:T(8,128)S(1)} %get-tuple-element.19), channel_id=1, source_target_pairs={{0,1},{1,0},{2,3},{3,2},{4,5},{5,4},{6,7},{7,6},{8,9},{9,8},{10,11... | collective-permute-start | bytes 24584 | tf_op jit(solution)/shard_map/ppermute | solution.py:509
  8.5 4.0 %collective-permute-start.4 = (f32[2,8,128]{2,1,0:T(8,128)S(1)}, f32[2,8,128]{2,1,0:T(8,128)S(1)}, u32[]{:S(2)}, u32[]{:S(2)}) collective-permute-start(f32[2,8,128]{2,1,0:T(8,128)S(1)} %get-tuple-element.19), channel_id=1, source_target_pairs={{1,2},{2,1},{5,6},{6,5},{9,10},{10,9},{13,14},{14,13},{17,18},{18,... | collective-permute-start | bytes 24584 | tf_op jit(solution)/shard_map/ppermute | solution.py:509

commit v2 on v1

--- a/solution.py
+++ b/solution.py
@@ -133,6 +133,10 @@
 def pick_k(axis, load):
     one, two = DIFFS[axis]
     return [load(6 + YZ), load(6 + XZ), load(6 + XY), load(6 + one) - load(6 + two)]
+
+
+def upward(place, slots, slot):
+    return place == 0 if slots == 1 else jnp.asarray(slot == 0)
 
 
 def faces_kernel(slots, metric, curvature, *refs):
@@ -169,7 +173,7 @@
     lanes = iota(slab, 1).astype(jnp.float32)
     z = lanes + z0
     for slot in range(nx):
-        high = (ix % 2) == slot
+        high = upward(ix, nx, slot)
         near_at = jnp.where(high, BLK + 1, 2)
         far_at = jnp.where(high, BLK, 3)
         sign = jnp.where(high, -1.0, 1.0)
@@ -188,7 +192,7 @@
             x_out[slot][0, layer] = real
             x_out[slot][1, layer] = imag
     for slot in range(ny):
-        high = (iy % 2) == slot
+        high = upward(iy, ny, slot)
         near_at = jnp.where(high, 8 + BLK - 1, 8)
         far_at = jnp.where(high, 8 + BLK - 2, 9)
         sign = jnp.where(high, -1.0, 1.0)
@@ -390,6 +394,12 @@
     copy.wait()
 
 
+def below(place, slots, slot, axis):
+    if slots == 1:
+        return place == 1, jnp.asarray(True)
+    return jnp.asarray(slot == 0), (place > 0 if slot == 0 else place < lax.axis_size(axis) - 1)
+
+
 def finish_kernel(slots, local, *refs):
     nx, ny, nz = slots
     x_in = refs[:nx]
@@ -402,35 +412,29 @@
     lane = iota((8, 128), 1)
     q = lane % 4
     edge = (lane >= 126) | (lane < 2)
+    upper = q < 2
+    held = jnp.where(upper, (iz < lax.axis_size("gz") - 1).astype(jnp.int32), (iz > 0).astype(jnp.int32)) == 1
     for part in range(2):
-        got = [ref[part] for ref in z_in]
-        if nz == 1:
-            got = got * 2
-        even = (iz % 2) == 0
-        plus = jnp.where(even, got[0], got[1])
-        less = jnp.where(even, got[1], got[0])
-        z_part = jnp.where(q < 2, plus, less)
-        if nz == 1:
-            z_part = jnp.where((q < 2) == even, got[0], 0.0)
-        z_part = z_part - z_fix[part]
+        z_part = jnp.where(upper, z_in[-1][part], z_in[0][part])
+        z_part = jnp.where(held, z_part, 0.0) - z_fix[part]
         for j in range(32):
             moved = pltpu.roll(z_part, (126 - 4 * j) % 128, 1)
             value = local[part, j // 2, pl.ds(8 * (j % 2), 8), :]
             work[part, pl.ds(8 * j, 8), :] = value + jnp.where(edge, moved, 0.0)
     for part in range(2):
         for slot in range(nx):
-            high = (ix % 2) == slot
+            low, real = below(ix, nx, slot, "gx")
             for layer in range(2):
-                at = jnp.where(high, BLK - 1 - layer, layer) * BLK
+                at = jnp.where(low, layer, BLK - 1 - layer) * BLK
                 span = pl.ds(pl.multiple_of(at, BLK), BLK)
-                work[part, span, :] = work[part, span, :] + x_in[slot][part, layer]
+                work[part, span, :] = work[part, span, :] + jnp.where(real, x_in[slot][part, layer], 0.0)
         for slot in range(ny):
-            high = (iy % 2) == slot
+            low, real = below(iy, ny, slot, "gy")
             for layer in range(2):
-                at = jnp.where(high, BLK - 1 - layer, layer)
+                at = jnp.where(low, layer, BLK - 1 - layer)
                 span = pl.ds(part * 256 + at, BLK, stride=BLK)
                 both = work.reshape(512, 128)
-                both[span, :] = both[span, :] + y_in[slot][part, layer]
+                both[span, :] = both[span, :] + jnp.where(real, y_in[slot][part, layer], 0.0)
     row = iota((8, 128), 0)
     source = (lane // BLK + row + 1) % 8
     for part in range(2):
@@ -472,11 +476,10 @@
     copy.wait()
 
 
-def matching(axis, slot):
-    perm = []
-    for low in range(slot, lax.axis_size(axis) - 1, 2):
-        perm += [(low, low + 1), (low + 1, low)]
-    return perm
+def shift(axis, slot):
+    count = lax.axis_size(axis)
+    step = 1 - 2 * slot
+    return [(place, (place + step) % count) for place in range(count)]
 
 
 def shards(metric_pert, curvature, interp_weights, point_ids, theta, phi):
@@ -504,9 +507,9 @@
     )(far(metric_pert), far(curvature))
     x_send, y_send = first[:nx], first[nx : nx + ny]
     z_send, z_fix, fields = first[nx + ny :]
-    x_got = [lax.ppermute(x_send[slot], "gx", matching("gx", slot)) for slot in range(nx)]
-    y_got = [lax.ppermute(y_send[slot], "gy", matching("gy", slot)) for slot in range(ny)]
-    z_got = [lax.ppermute(z_send, "gz", matching("gz", slot)) for slot in range(nz)]
+    x_got = [lax.ppermute(x_send[slot], "gx", shift("gx", slot)) for slot in range(nx)]
+    y_got = [lax.ppermute(y_send[slot], "gy", shift("gy", slot)) for slot in range(ny)]
+    z_got = [lax.ppermute(z_send, "gz", shift("gz", slot)) for slot in range(nz)]
     weights = interp_weights.reshape(count, cells)
     local, harm, ids, loaded = pl.pallas_call(
         interior_kernel,

time: 31.8 us -> 30 us (0.943)
  blocking collectives: 15.8 us -> 11.6 us
  starting transfers between devices: 5.98 us -> 8.6 us
    all_to_all x1, blocking collectives: 15.8 us -> 11.6 us  [shards(): modes = lax.all_to_all(modes, AXES, 0, 0, tiled=True).sum(0)]
    ppermute x5, starting transfers between devices: 5.98 us -> 8.6 us  [the longest x2 3.82 us: shards(): lax.ppermute(z_send, 'gz', shift('gz', slot))]
where the time goes in v2:
time: 30 us; the launch traced here: 29.9 us
  blocking collectives  11.6 us (39%)
  starting transfers between devices  8.6 us (29%)
  Pallas kernels  8.37 us (28%)
  between operations  0.7 us (2%)
  local copies, waits for them, and re-layouts  0.59 us (2%)
    all_to_all x1, blocking collectives, shards(): modes = lax.all_to_all(modes, AXES, 0, 0, tiled=True).sum(0)  11.6 us
    ppermute x2, starting transfers between devices, shards(): lax.ppermute(z_send, 'gz', shift('gz', slot))  3.82 us
    pallas_call x1, Pallas kernels, shards(): pl.pallas_call(interior_kernel, out_shape=[VMEM((2, BLK, BLK, 128), f32),...  3.33 us
    ppermute x1, starting transfers between devices, shards(): lax.ppermute(x_send[slot], 'gx', shift('gx', slot))  3.03 us
    pallas_call x1, Pallas kernels, shards(): pl.pallas_call(functools.partial(finish_kernel, slots), out_shape=[pltpu....  2.63 us
    pallas_call x1, Pallas kernels, shards(): pl.pallas_call(functools.partial(faces_kernel, slots), out_shape=[face] *...  2.41 us
    ppermute x2, starting transfers between devices, shards(): lax.ppermute(y_send[slot], 'gy', shift('gy', slot))  1.75 us
  transfers between devices with their start and end apart: 5, of which 0 were waited for; matrix products, arithmetic and copies ran while one was open for 0% of the time, Pallas kernels for 11%

profile of v2, /device:TPU:0, one launch (start us, length us, event | category | flops | bytes accessed | tf_op | source)
XLA Modules:
  0.0 29.9 jit_solution(455329054186965577)
XLA Ops:
  0.6 2.4 %faces.1 = (f32[2,2,16,128]{3,2,1,0:T(8,128)S(1)}, f32[2,2,16,128]{3,2,1,0:T(8,128)S(1)}, f32[2,2,16,128]{3,2,1,0:T(8,128)S(1)}, f32[2,8,128]{2,1,0:T(8,128)S(1)...) custom-call(f32[6,16,16,128]{3,2,1,0:T(8,128)} %metric.1, f32[6,16,16,128]{3,2,1,0:T(8,128)} %curvature.1), custom_call_target="tpu_custom_call" | custom-call | tf_op jit(solution)/shard_map/faces/pallas_call | solution.py:499
  3.0 3.0 %collective-permute-start = (f32[2,2,16,128]{3,2,1,0:T(8,128)S(1)}, f32[2,2,16,128]{3,2,1,0:T(8,128)S(1)}, u32[]{:S(2)}, u32[]{:S(2)}) collective-permute-start(f32[2,2,16,128]{3,2,1,0:T(8,128)S(1)} %get-tuple-element.16), channel_id=1, source_target_pairs={{0,16},{16,0},{1,17},{17,1},{2,18},{18,2},{3,19},{19,3},{4,20},{20... | collective-permute-start | bytes 98312 | tf_op jit(solution)/shard_map/ppermute | solution.py:510
  6.1 0.0 collective-permute-start.1
  6.1 1.7 %collective-permute-start.2 = (f32[2,2,16,128]{3,2,1,0:T(8,128)S(1)}, f32[2,2,16,128]{3,2,1,0:T(8,128)S(1)}, u32[]{:S(2)}, u32[]{:S(2)}) collective-permute-start(f32[2,2,16,128]{3,2,1,0:T(8,128)S(1)} %get-tuple-element.18), channel_id=1, source_target_pairs={{0,12},{4,0},{8,4},{12,8},{1,13},{5,1},{9,5},{13,9},{2,14},{6,2},{... | collective-permute-start | bytes 98312 | tf_op jit(solution)/shard_map/ppermute | solution.py:511
  7.8 1.6 %collective-permute-start.3 = (f32[2,8,128]{2,1,0:T(8,128)S(1)}, f32[2,8,128]{2,1,0:T(8,128)S(1)}, u32[]{:S(2)}, u32[]{:S(2)}) collective-permute-start(f32[2,8,128]{2,1,0:T(8,128)S(1)} %get-tuple-element.19), channel_id=1, source_target_pairs={{0,1},{1,2},{2,3},{3,0},{4,5},{5,6},{6,7},{7,4},{8,9},{9,10},{10,1... | collective-permute-start | bytes 24584 | tf_op jit(solution)/shard_map/ppermute | solution.py:512
  9.4 2.2 %collective-permute-start.4 = (f32[2,8,128]{2,1,0:T(8,128)S(1)}, f32[2,8,128]{2,1,0:T(8,128)S(1)}, u32[]{:S(2)}, u32[]{:S(2)}) collective-permute-start(f32[2,8,128]{2,1,0:T(8,128)S(1)} %get-tuple-element.19), channel_id=1, source_target_pairs={{0,3},{1,0},{2,1},{3,2},{4,7},{5,4},{6,5},{7,6},{8,11},{9,8},{10,9... | collective-permute-start | bytes 24584 | tf_op jit(solution)/shard_map/ppermute | solution.py:512
  11.6 3.3 %interior.1 = (f32[2,16,16,128]{3,2,1,0:T(8,128)S(1)}, f32[80,1024]{1,0:T(8,128)S(1)}, s32[1,512]{1,0:T(1,128)S(1)}, bf16[512,4096]{1,0:T(8,128)(2,1)S(1)}) custom-call(f32[12,20,32,128]{3,2,1,0:T(8,128)S(1)} %get-tuple-element.14.fields, s32[8,64]{1,0:T(8,128)} %bitcast.9, f32[48,128]{1,0:T(8,128)} %bitcast.6, f32[48,128]{1,0:T(8,128)} %bitcast.7, ...), custom_call_target="tpu_custom_call" | custom-call | flops 20000000 | bytes 8000000 | tf_op jit(solution)/shard_map/interior/pallas_call | solution.py:514
  15.0 0.0 collective-permute-done.3.refs_3_
  15.0 0.0 collective-permute-done.4.refs_4_
  15.0 0.0 collective-permute-done.refs_0_
  15.0 0.0 collective-permute-done.1.refs_1_
  15.0 0.0 collective-permute-done.2.refs_2_
  15.0 2.6 %finish.1 = (bf16[2,16,16,128]{3,2,1,0:T(8,128)(2,1)}, f32[32,8,128]{2,1,0:T(8,128)S(1)}) custom-call(f32[2,16,16,128]{3,2,1,0:T(8,128)S(1)} %get-tuple-element.15.local, f32[2,2,16,128]{3,2,1,0:T(8,128)S(1)} %collective-permute-done.refs_0_, f32[2,2,16,128]{3,2,1,0:T(8,128)S(1)} %collective-permute-done.1.refs_1_, ...), custom_call_target="tpu_custom_call" | custom-call | tf_op jit(solution)/shard_map/finish/pallas_call | solution.py:538
  17.7 11.6 %all_to_all.5 = f32[32,8,128]{2,1,0:T(8,128)S(1)} all-to-all(f32[32,8,128]{2,1,0:T(8,128)S(1)} %get-tuple-element.25), channel_id=1, replica_groups=mesh['gx'=2,'gy'=4,'gz'=4] {'gx','gy','gz'}, dimensions={0} | all-to-all | bytes 262144 | tf_op jit(solution)/shard_map/all_to_all | solution.py:552
  29.3 0.6 %reshape.23 = f32[3,2,77]{2,1,0:T(2,128)} reshape(f32[6,77]{1,0:T(8,128)S(1)} %bitcast.8) | data formatting | bytes 3696 | tf_op jit(solution)/shard_map/reshape | solution.py:553
  (1 shorter events, 0.0 us)
Async XLA Ops:
  3.0 12.0 %collective-permute-start = (f32[2,2,16,128]{3,2,1,0:T(8,128)S(1)}, f32[2,2,16,128]{3,2,1,0:T(8,128)S(1)}, u32[]{:S(2)}, u32[]{:S(2)}) collective-permute-start(f32[2,2,16,128]{3,2,1,0:T(8,128)S(1)} %get-tuple-element.16), channel_id=1, source_target_pairs={{0,16},{16,0},{1,17},{17,1},{2,18},{18,2},{3,19},{19,3},{4,20},{20... | collective-permute-start | bytes 98312 | tf_op jit(solution)/shard_map/ppermute | solution.py:510
  6.1 8.9 %collective-permute-start.1 = (f32[2,2,16,128]{3,2,1,0:T(8,128)S(1)}, f32[2,2,16,128]{3,2,1,0:T(8,128)S(1)}, u32[]{:S(2)}, u32[]{:S(2)}) collective-permute-start(f32[2,2,16,128]{3,2,1,0:T(8,128)S(1)} %get-tuple-element.17), channel_id=1, source_target_pairs={{0,4},{4,8},{8,12},{12,0},{1,5},{5,9},{9,13},{13,1},{2,6},{6,10},{... | collective-permute-start | bytes 98312 | tf_op jit(solution)/shard_map/ppermute | solution.py:511
  6.1 9.0 %collective-permute-start.2 = (f32[2,2,16,128]{3,2,1,0:T(8,128)S(1)}, f32[2,2,16,128]{3,2,1,0:T(8,128)S(1)}, u32[]{:S(2)}, u32[]{:S(2)}) collective-permute-start(f32[2,2,16,128]{3,2,1,0:T(8,128)S(1)} %get-tuple-element.18), channel_id=1, source_target_pairs={{0,12},{4,0},{8,4},{12,8},{1,13},{5,1},{9,5},{13,9},{2,14},{6,2},{... | collective-permute-start | bytes 98312 | tf_op jit(solution)/shard_map/ppermute | solution.py:511
  7.8 7.2 %collective-permute-start.3 = (f32[2,8,128]{2,1,0:T(8,128)S(1)}, f32[2,8,128]{2,1,0:T(8,128)S(1)}, u32[]{:S(2)}, u32[]{:S(2)}) collective-permute-start(f32[2,8,128]{2,1,0:T(8,128)S(1)} %get-tuple-element.19), channel_id=1, source_target_pairs={{0,1},{1,2},{2,3},{3,0},{4,5},{5,6},{6,7},{7,4},{8,9},{9,10},{10,1... | collective-permute-start | bytes 24584 | tf_op jit(solution)/shard_map/ppermute | solution.py:512
  9.4 5.6 %collective-permute-start.4 = (f32[2,8,128]{2,1,0:T(8,128)S(1)}, f32[2,8,128]{2,1,0:T(8,128)S(1)}, u32[]{:S(2)}, u32[]{:S(2)}) collective-permute-start(f32[2,8,128]{2,1,0:T(8,128)S(1)} %get-tuple-element.19), channel_id=1, source_target_pairs={{0,3},{1,0},{2,1},{3,2},{4,7},{5,4},{6,5},{7,6},{8,11},{9,8},{10,9... | collective-permute-start | bytes 24584 | tf_op jit(solution)/shard_map/ppermute | solution.py:512

commit v3 on v1

v3 whole, which is shorter than its diff:
```python
import functools
import math

import jax
import jax.numpy as jnp
import numpy as np
from jax import lax
from jax.experimental import pallas as pl
from jax.experimental.pallas import tpu as pltpu
from jax.sharding import PartitionSpec as P

BLK = 16
PTS = 2048
SPHERES = 3
LMAX = 8
AXES = ("gx", "gy", "gz")
MODES = (LMAX + 1) ** 2 - 4
ROWS = 24
NEAR = 1.0 / 3.0
FAR = 1.0 / 24.0
XX, XY, XZ, YY, YZ, ZZ = range(6)
VMEM = pltpu.VMEM
LIMIT = 24 * 1024 * 1024


def recurrence():
    table = np.zeros((ROWS, 128), np.float32)
    norm = lambda degree: math.sqrt((2 * degree + 1) / (4.0 * math.pi))
    for order in range(-LMAX, LMAX + 1):
        low = max(2, abs(order))
        row = order + LMAX
        gap = lambda degree: math.sqrt((degree**2 - order**2) * (degree**2 - 4))
        for degree in range(low, LMAX):
            base = 3 * (degree - 2)
            lift = degree * gap(degree + 1)
            scale = norm(degree + 1) / norm(degree) * (2 * degree + 1) / lift
            table[row, base] = scale * degree * (degree + 1)
            table[row, base + 1] = -scale * 2 * order
            if degree > low:
                table[row, base + 2] = norm(degree + 1) / norm(degree - 1) * (degree + 1) * gap(degree) / lift
        step = min(max(order, -2), 2) + 2 if low == 2 else (low + 2 if order > 0 else 0)
        lower = step - 2 - order
        lead = (-1.0) ** order * math.sqrt(
            math.factorial(low + order)
            * math.factorial(low - order)
            * (2 * low + 1)
            / (4.0 * math.pi * math.factorial(low - 2) * math.factorial(low + 2))
        )
        table[row, 127] = lead * math.comb(low + 2, step) * math.comb(low - 2, lower) * (-1.0) ** (low - step + 2)
    return table


def frame(x, y, z):
    rho2 = x * x + y * y
    inv_rho = lax.rsqrt(rho2)
    inv_r = lax.rsqrt(rho2 + z * z)
    cos_p = x * inv_rho
    sin_p = y * inv_rho
    cos_t = z * inv_r
    sin_t = rho2 * inv_rho * inv_r
    cc = cos_p * cos_p
    ss = sin_p * sin_p
    tt = cos_t * cos_t
    cs = cos_p * sin_p
    st = sin_t * cos_t
    twice_p = (tt * cc - ss, cs * (tt + 1.0), -(st * cos_p), tt * ss - cc, -(st * sin_p), sin_t * sin_t)
    q_diag = cos_t * cs
    twice_q = (cos_t * (cc - ss), sin_t * sin_p, -(sin_t * cos_p))
    return twice_p, q_diag, twice_q


def total(terms):
    terms = [term for term in terms if term is not None]
    return functools.reduce(lambda one, two: one + two, terms)


def times(one, two):
    return None if one is None or two is None else one * two


def minus(one, two):
    if two is None:
        return one
    return -two if one is None else one - two


def contract(geometry, electric, magnetic):
    twice_p, q_diag, twice_q = geometry
    e, b = electric, magnetic
    off = (XY, XZ, YZ)
    real_e = (twice_p[XX] * e[0] + twice_p[YY] * e[1]) * 0.5
    real_e = real_e + total([twice_p[i] * e[2 + n] for n, i in enumerate(off)])
    imag_e = q_diag * (e[1] - e[0]) + total([twice_q[n] * e[2 + n] for n in range(3)])
    real_b = total([times(2.0 * q_diag, minus(b[YY], b[XX]))] + [times(twice_q[n], b[i]) for n, i in enumerate(off)])
    imag_b = total([times(twice_p[i], b[i]) for i in range(6)])
    return real_e - real_b, -(imag_e + imag_b)


def curl_part(axis, d):
    yz, xz, xy, diff = d
    if axis == 0:
        return [None, -xz, xy, -yz, diff, yz]
    if axis == 1:
        return [xz, yz, diff, None, -xy, -xz]
    return [-xy, diff, -yz, xy, xz, None]


H_PARTS = (XX, YY, XY, XZ, YZ)
DIFFS = ((YY, ZZ), (ZZ, XX), (XX, YY))


def iota(shape, dim):
    return lax.broadcasted_iota(jnp.int32, shape, dim)


def origin(axis, cells):
    place = lax.axis_index(axis)
    count = lax.axis_size(axis)
    return (place * cells).astype(jnp.float32) + (0.5 - count * cells / 2.0), place


def face_part(axis, near, far, sign, geometry):
    h_near, k_near = near if near is not None else (None, None)
    h_far, k_far = far
    if near is None:
        e = [h * FAR for h in h_far]
        d = [k * (-FAR * sign) for k in k_far]
    else:
        e = [f * FAR - n * (2.0 / 3.0) for n, f in zip(h_near, h_far)]
        d = [(n * NEAR - f * FAR) * sign for n, f in zip(k_near, k_far)]
    return contract(geometry, e, curl_part(axis, d))


def pick_k(axis, load):
    one, two = DIFFS[axis]
    return [load(6 + YZ), load(6 + XZ), load(6 + XY), load(6 + one) - load(6 + two)]


def sin_cos(x):
    x2 = x * x
    sine = 0.0
    cosine = 0.0
    for n in range(6, -1, -1):
        sine = sine * x2 + (-1.0) ** n / math.factorial(2 * n + 1)
    for n in range(7, -1, -1):
        cosine = cosine * x2 + (-1.0) ** n / math.factorial(2 * n)
    return sine * x, cosine


def split3(value):
    one = value.astype(jnp.bfloat16)
    rest = value - one.astype(jnp.float32)
    two = rest.astype(jnp.bfloat16)
    three = (rest - two.astype(jnp.float32)).astype(jnp.bfloat16)
    return one, two, three


def harmonics(lists, theta, phi, coefs, plain, harm, ids):
    count = ids.shape[1]
    id_row = jnp.concatenate([lists[n : n + 1] for n in range(lists.shape[0])], axis=1)
    ids[...] = id_row
    wide = (theta.shape[0], count)
    pick = jnp.where(iota(wide, 0) == id_row // 128, 1.0, 0.0).astype(jnp.bfloat16)
    tables = jnp.concatenate([theta[...], phi[...]], axis=1)
    left = jnp.concatenate(split3(tables), axis=0)
    right = jnp.concatenate([pick] * 3, axis=0)
    found = lax.dot_general(left, right, (((0,), (0,)), ((), ())), preferred_element_type=jnp.float32)
    mine = iota((128, count), 0) == id_row % 128
    half_t = jnp.sum(jnp.where(mine, found[:128], 0.0), axis=0, keepdims=True) * 0.5
    half_p = jnp.sum(jnp.where(mine, found[128:], 0.0), axis=0, keepdims=True) * 0.5
    sines, cosines = sin_cos(jnp.concatenate([half_t, half_p, jnp.zeros((6, count), jnp.float32)], axis=0))
    sin_h, cos_h = sines[0:1], cosines[0:1]
    cos_t = cos_h * cos_h - sin_h * sin_h
    sin_p = 2.0 * sines[1:2] * cosines[1:2]
    cos_p = 1.0 - 2.0 * sines[1:2] * sines[1:2]
    shape = (ROWS, count)
    order = iota(shape, 0) - LMAX
    size = jnp.abs(order)
    lowest = jnp.maximum(size, 2)
    tilt = jnp.clip(order, -2, 2)
    unit_r = jnp.ones(shape, jnp.float32)
    unit_i = jnp.zeros(shape, jnp.float32)
    start = jnp.where(size <= LMAX, coefs[:, 127:128], 0.0)
    step_r, step_i, step_c, step_s = cos_p, sin_p, cos_h, sin_h
    for bit in range(4):
        has = (size >> bit) & 1 == 1
        new_r = unit_r * step_r - unit_i * step_i
        new_i = unit_r * step_i + unit_i * step_r
        unit_r = jnp.where(has, new_r, unit_r)
        unit_i = jnp.where(has, new_i, unit_i)
        start = jnp.where(((lowest + tilt) >> bit) & 1 == 1, start * step_c, start)
        start = jnp.where(((lowest - tilt) >> bit) & 1 == 1, start * step_s, start)
        step_r, step_i = step_r * step_r - step_i * step_i, 2.0 * step_r * step_i
        step_c = step_c * step_c
        step_s = step_s * step_s
    unit_i = jnp.where(order < 0, -unit_i, unit_i)
    before = jnp.zeros(shape, jnp.float32)
    now = jnp.where(lowest == 2, start, 0.0)
    for degree in range(2, LMAX + 1):
        if degree > 2:
            base = 3 * (degree - 3)
            slope = coefs[:, base : base + 1] * cos_t + coefs[:, base + 1 : base + 2]
            after = slope * now - coefs[:, base + 2 : base + 3] * before
            before, now = now, jnp.where(lowest == degree, start, after)
        at = degree * degree - 4
        width = 2 * degree + 1
        low = LMAX - degree
        plain[pl.ds(at, width), pl.ds(0, count)] = (now * unit_r)[low : low + width]
        plain[pl.ds(at, width), pl.ds(count, count)] = (now * unit_i)[low : low + width]
    plain[pl.ds(MODES, 80 - MODES), :] = jnp.zeros((80 - MODES, 2 * count), jnp.float32)
    whole = plain[...]
    main = whole.astype(jnp.bfloat16)
    harm[0] = main
    harm[1] = (whole - main.astype(jnp.float32)).astype(jnp.bfloat16)


def faces_kernel(slots, metric, curvature, ids_far, theta_far, phi_far, coefs_far, *refs):
    nx, ny, _ = slots
    x_out = refs[:nx]
    y_out = refs[nx : nx + ny]
    z_out, z_fix, fields, harm, ids, lists, theta, phi, coefs, plain, sems = refs[nx + ny :]
    small = [
        pltpu.make_async_copy(source, target, sems.at[n])
        for n, (source, target) in enumerate(
            ((ids_far, lists), (theta_far, theta), (phi_far, phi), (coefs_far, coefs))
        )
    ]
    copies = []
    for base, source in ((0, metric), (6, curvature)):
        copies.append(
            pltpu.make_async_copy(
                source,
                fields.at[pl.ds(base, 6), pl.ds(2, BLK), pl.ds(8, BLK), :],
                sems.at[4 + base // 6],
            )
        )
    for copy in small + copies:
        copy.start()
    blank = jnp.zeros((12, BLK, 8, 128), jnp.float32)
    fields[:, pl.ds(2, BLK), pl.ds(0, 8), :] = blank
    fields[:, pl.ds(2, BLK), pl.ds(24, 8), :] = blank
    plane = jnp.zeros((12, 2, BLK, 128), jnp.float32)
    fields[:, pl.ds(0, 2), pl.ds(8, BLK), :] = plane
    fields[:, pl.ds(BLK + 2, 2), pl.ds(8, BLK), :] = plane
    for copy in small:
        copy.wait()
    harmonics(lists, theta, phi, coefs, plain, harm, ids)
    for copy in copies:
        copy.wait()
    inside = (pl.ds(2, BLK), pl.ds(8, BLK), slice(None))
    h_zz = fields[(ZZ, *inside)]
    fields[(XX, *inside)] = fields[(XX, *inside)] - h_zz
    fields[(YY, *inside)] = fields[(YY, *inside)] - h_zz
    x0, ix = origin("gx", BLK)
    y0, iy = origin("gy", BLK)
    z0, iz = origin("gz", 128)
    slab = (BLK, 128)
    rows = iota(slab, 0).astype(jnp.float32)
    lanes = iota(slab, 1).astype(jnp.float32)
    z = lanes + z0

    def facing(axis, load, near_at, far_at, sign, geometry_at):
        near = [load(c, near_at) for c in H_PARTS]
        far = [load(c, far_at) for c in H_PARTS]
        k_near = pick_k(axis, lambda c: load(c, near_at))
        k_far = pick_k(axis, lambda c: load(c, far_at))
        return (
            face_part(axis, (near, k_near), (far, k_far), sign, geometry_at(0)),
            face_part(axis, None, (near, k_near), sign, geometry_at(1)),
        )

    def send(axis, place, outs, load, last, start, geometry):
        even = place % 2 == 0
        if len(outs) == 1:
            sides = [
                facing(
                    axis,
                    load,
                    jnp.where(even, last, 0),
                    jnp.where(even, last - 1, 1),
                    jnp.where(even, -1.0, 1.0),
                    lambda layer: geometry(jnp.where(even, start + (BLK + layer), start - (1 + layer))),
                )
            ]
        else:
            high = facing(axis, load, last, last - 1, -1.0, lambda layer: geometry(start + (BLK + layer)))
            low = facing(axis, load, 0, 1, 1.0, lambda layer: geometry(start - (1 + layer)))
            pick = lambda one, two: jax.tree.map(lambda a, b: jnp.where(even, a, b), one, two)
            sides = [pick(high, low), pick(low, high)]
        for out, side in zip(outs, sides):
            for layer in range(2):
                for part in range(2):
                    out[part, layer] = side[layer][part]

    flat = fields.reshape(12 * 20 * 32, 128)
    send(
        0,
        ix,
        x_out,
        lambda c, at: fields[c, 2 + at, pl.ds(8, BLK), :],
        BLK - 1,
        x0,
        lambda x: frame(x, rows + y0, z),
    )
    send(
        1,
        iy,
        y_out,
        lambda c, at: flat[pl.ds(c * 640 + 72 + at, BLK, stride=32), :],
        BLK - 1,
        y0,
        lambda y: frame(rows + x0, y, z),
    )
    lane = iota((8, 128), 1)
    group = lane // 4

    def packed(load):
        out = jnp.zeros((8, 128), jnp.float32)
        for j in range(32):
            value = load(j // 2, j % 2)
            out = jnp.where(group == j, pltpu.roll(value, (2 + 4 * j) % 128, 1), out)
        return out

    def piece(c):
        return lambda x, half: fields[c, 2 + x, pl.ds(8 + 8 * half, 8), :]

    h_all = [packed(piece(c)) for c in H_PARTS]
    one, two = DIFFS[2]
    k_all = [packed(piece(6 + c)) for c in (YZ, XZ, XY)]
    k_all.append(packed(lambda x, half: piece(6 + one)(x, half) - piece(6 + two)(x, half)))
    q = lane % 4
    upper = q >= 2
    inner = (q == 1) | (q == 2)

    def shifted(value, by):
        return jnp.where(upper, pltpu.roll(value, by, 1), pltpu.roll(value, 128 - by, 1))

    e = [shifted(h, 2) * FAR - jnp.where(inner, shifted(h, 1), 0.0) * (2.0 / 3.0) for h in h_all]
    sign = jnp.where(upper, -1.0, 1.0)
    d = [(jnp.where(inner, shifted(k, 1), 0.0) * NEAR - shifted(k, 2) * FAR) * sign for k in k_all]
    magnetic = curl_part(2, d)
    x = (lane // 8).astype(jnp.float32) + x0
    y = (iota((8, 128), 0) + 8 * (group % 2)).astype(jnp.float32) + y0
    z_here = jnp.where(upper, q - 2, q + 126).astype(jnp.float32) + z0
    z_there = z_here + jnp.where(upper, 128.0, -128.0)
    for out, z_at in ((z_out, z_there), (z_fix, z_here)):
        real, imag = contract(frame(x, y, z_at), e, magnetic)
        out[0] = real
        out[1] = imag


def interior_kernel(fields, weights, local, loaded, sem):
    copy = pltpu.make_async_copy(weights, loaded, sem)
    copy.start()
    x0, _ = origin("gx", BLK)
    y0, _ = origin("gy", BLK)
    z0, _ = origin("gz", 128)
    slab = (BLK, 128)
    y = iota(slab, 0).astype(jnp.float32) + y0
    z = iota(slab, 1).astype(jnp.float32) + z0

    def plane(i, carry):
        def at(c, dx=0, dy=0):
            return fields[c, i + (2 + dx), pl.ds(8 + dy, BLK), :]

        def roll(value, by):
            return pltpu.roll(value, by % 128, 1)

        geometry = frame(x0 + i.astype(jnp.float32), y, z)
        k = [at(6 + c) for c in range(6)]
        trace = k[XX] + k[YY] + k[ZZ]
        xx, xy, xz, yy, yz, zz = [value * value for value in k]
        left = xy - zz
        squares = (
            xx - yz + left,
            yy - xz + left,
            k[XY] * (k[XX] + k[YY]) + k[XZ] * k[YZ],
            k[XZ] * (k[XX] + k[ZZ]) + k[XY] * k[YZ],
            k[YZ] * (k[YY] + k[ZZ]) + k[XY] * k[XZ],
        )
        linear = (k[XX] - k[ZZ], k[YY] - k[ZZ], k[XY], k[XZ], k[YZ])
        e = []
        for n, c in enumerate(H_PARTS):
            h = at(c)
            one = (at(c, -1) + at(c, 1)) + (at(c, 0, -1) + at(c, 0, 1)) + (roll(h, 1) + roll(h, -1))
            two = (at(c, -2) + at(c, 2)) + (at(c, 0, -2) + at(c, 0, 2)) + (roll(h, 2) + roll(h, -2))
            e.append(two * FAR - one * (2.0 / 3.0) + h * 3.75 + (trace * linear[n] - squares[n]))

        def slope(m2, m1, p1, p2):
            return (p1 - m1) * NEAR - (p2 - m2) * FAR

        steps = (-2, -1, 1, 2)
        along_x = [pick_k(0, lambda c, s=s: at(c, s)) for s in steps]
        dx = [slope(*[along_x[n][f] for n in range(4)]) for f in range(4)]
        along_y = [pick_k(1, lambda c, s=s: at(c, 0, s)) for s in steps]
        dy = [slope(*[along_y[n][f] for n in range(4)]) for f in range(4)]
        here = [k[YZ], k[XZ], k[XY], k[XX] - k[YY]]
        dz = [slope(*[roll(f, -s) for s in steps]) for f in here]
        parts = [curl_part(axis, d) for axis, d in enumerate((dx, dy, dz))]
        magnetic = [total([part[c] for part in parts]) for c in range(6)]
        real, imag = contract(geometry, e, magnetic)
        local[0, i] = real
        local[1, i] = imag
        return carry

    lax.fori_loop(0, BLK, plane, 0, unroll=2)
    copy.wait()


def transposed_dot(one, two):
    return lax.dot_general(one, two, (((1,), (1,)), ((), ())), preferred_element_type=jnp.float32)


def arrived(place, axis, refs, at):
    even = place % 2 == 0
    one, two = refs[0][at], refs[-1][at]
    before = jnp.where(place > 0, jnp.where(even, two, one), 0.0)
    after = jnp.where(place < lax.axis_size(axis) - 1, jnp.where(even, one, two), 0.0)
    return before, after


def finish_kernel(slots, local, *refs):
    nx, ny, nz = slots
    x_in = refs[:nx]
    y_in = refs[nx : nx + ny]
    z_in = refs[nx + ny : nx + ny + nz]
    z_fix, weights, harm, ids, psi, modes, work, stored, flat, sem = refs[nx + ny + nz :]
    ix = lax.axis_index("gx")
    iy = lax.axis_index("gy")
    iz = lax.axis_index("gz")
    lane = iota((8, 128), 1)
    q = lane % 4
    edge = (lane >= 126) | (lane < 2)
    for part in range(2):
        before, after = arrived(iz, "gz", z_in, part)
        z_part = jnp.where(q < 2, after, before) - z_fix[part]
        for j in range(32):
            moved = pltpu.roll(z_part, (126 - 4 * j) % 128, 1)
            value = local[part, j // 2, pl.ds(8 * (j % 2), 8), :]
            work[part, pl.ds(8 * j, 8), :] = value + jnp.where(edge, moved, 0.0)
    both = work.reshape(512, 128)
    for part in range(2):
        for layer in range(2):
            for place, axis, refs, stride in ((ix, "gx", x_in, 1), (iy, "gy", y_in, BLK)):
                for side, at in zip(arrived(place, axis, refs, (part, layer)), (layer, BLK - 1 - layer)):
                    first = 256 * part + at * (BLK // stride)
                    span = pl.ds(first, BLK, stride=stride) if stride > 1 else pl.ds(first, BLK)
                    both[span, :] = both[span, :] + side
    row = iota((8, 128), 0)
    source = (lane // BLK + row + 1) % 8
    for part in range(2):
        for x in range(BLK):
            rounded = work[part, pl.ds(BLK * x, BLK), :].astype(jnp.bfloat16)
            stored[part, x] = rounded
            values = rounded.astype(jnp.float32)
            for half in range(2):
                value = values[8 * half : 8 * half + 8]
                value = pltpu.roll(value, 0, 1, stride=BLK, stride_axis=0)
                value = jnp.take_along_axis(value, source, axis=0)
                value = pltpu.roll(value, BLK, 1, stride=BLK, stride_axis=0)
                flat[pl.ds(8 * part, 8), pl.ds((2 * x + half) * 128, 128)] = value
    copy = pltpu.make_async_copy(stored, psi, sem)
    copy.start()
    count = ids.shape[1]
    blocks = flat[...].astype(jnp.bfloat16)
    product = transposed_dot(blocks, weights[...])
    own = iota((8, count), 0) == 7 - iota((8, count), 1) // (count // 8)
    real = jnp.sum(jnp.where(own, product[:8], 0.0), axis=0, keepdims=True)
    imag = jnp.sum(jnp.where(own, product[8:], 0.0), axis=0, keepdims=True)
    row = iota((8, count), 0)
    live = ids[...] // PTS == row // 2
    first = row % 2 == 0
    left = jnp.where(live, jnp.where(first, real, imag), 0.0)
    right = jnp.where(live, jnp.where(first, imag, -real), 0.0)
    points = jnp.concatenate([left, right], axis=1)
    main = points.astype(jnp.bfloat16)
    rest = (points - main.astype(jnp.float32)).astype(jnp.bfloat16)
    both = jnp.concatenate([main, rest], axis=0)
    sums = transposed_dot(both, harm[0])
    sums = sums[:8] + sums[8:] + transposed_dot(both, harm[1])[:8]
    sums = sums * (4.0 * math.pi / PTS)
    sums = jnp.concatenate([sums, jnp.zeros((8, 128 - 80), jnp.float32)], axis=1)
    modes[...] = jnp.broadcast_to(sums[None], modes.shape)
    copy.wait()


def swap(value, axis, slot, filler):
    sizes = [lax.axis_size(name) for name in AXES]
    along, aside = AXES.index(axis), AXES.index(filler)
    perm = []
    for place in np.ndindex(*sizes):
        other = list(place)
        other[along] += 1 if place[along] % 2 == slot else -1
        if not 0 <= other[along] < sizes[along]:
            other[along] = place[along]
            other[aside] ^= 1
            if other[aside] >= sizes[aside]:
                continue
        perm.append((int(np.ravel_multi_index(place, sizes)), int(np.ravel_multi_index(other, sizes))))
    return lax.ppermute(value, AXES, perm)


def shards(metric_pert, curvature, interp_weights, point_ids, theta, phi):
    f32 = jnp.float32
    hbm = pl.BlockSpec(memory_space=pltpu.HBM)
    far = lambda value: pltpu.with_memory_space_constraint(value, pltpu.HBM)
    close = lambda value: pltpu.with_memory_space_constraint(value, VMEM)
    vmem = pl.BlockSpec(memory_space=VMEM)
    slots = tuple(min(2, lax.axis_size(axis) - 1) for axis in AXES)
    nx, ny, nz = slots
    count = point_ids.size
    lists = point_ids.shape[2:]
    cells = BLK * BLK * BLK
    face = VMEM((2, 2, BLK, 128), f32)
    edge = VMEM((2, 8, 128), f32)
    params = pltpu.CompilerParams(vmem_limit_bytes=LIMIT)
    bf16 = jnp.bfloat16
    table = VMEM((theta.size // 128, 128), f32)
    first = pl.pallas_call(
        functools.partial(faces_kernel, slots),
        out_shape=[face] * (nx + ny)
        + [edge, edge, VMEM((12, 20, 32, 128), f32), VMEM((2, 80, 2 * count), bf16), VMEM((1, count), jnp.int32)],
        in_specs=[hbm] * 6,
        out_specs=[vmem] * (nx + ny + 5),
        scratch_shapes=[
            VMEM(lists, jnp.int32),
            table,
            table,
            VMEM((ROWS, 128), f32),
            VMEM((80, 2 * count), f32),
            pltpu.SemaphoreType.DMA((6,)),
        ],
        compiler_params=params,
        name="faces",
    )(
        far(metric_pert),
        far(curvature),
        far(point_ids.reshape(lists)),
        far(theta.reshape(-1, 128)),
        far(phi.reshape(-1, 128)),
        far(jnp.asarray(recurrence())),
    )
    x_send, y_send = first[:nx], first[nx : nx + ny]
    z_send, z_fix, fields, harm, ids = first[nx + ny :]
    x_got = [swap(x_send[slot], "gx", slot, "gy") for slot in range(nx)]
    y_got = [swap(y_send[slot], "gy", slot, "gx") for slot in range(ny)]
    z_got = [swap(z_send, "gz", slot, "gy") for slot in range(nz)]
    weights = interp_weights.reshape(count, cells)
    local, loaded = pl.pallas_call(
        interior_kernel,
        out_shape=[VMEM((2, BLK, BLK, 128), f32), VMEM((count, cells), bf16)],
        in_specs=[vmem, hbm],
        out_specs=[vmem] * 2,
        scratch_shapes=[pltpu.SemaphoreType.DMA],
        compiler_params=params,
        cost_estimate=pl.CostEstimate(flops=20_000_000, bytes_accessed=8_000_000, transcendentals=0),
        name="interior",
    )(close(fields), far(weights))
    total_devices = math.prod(lax.axis_size(axis) for axis in AXES)
    psi, modes = pl.pallas_call(
        functools.partial(finish_kernel, slots),
        out_shape=[pltpu.HBM((2, BLK, BLK, 128), jnp.bfloat16), VMEM((total_devices, 8, 128), f32)],
        in_specs=[vmem] * (1 + nx + ny + nz + 4),
        out_specs=[hbm, vmem],
        scratch_shapes=[
            VMEM((2, 256, 128), f32),
            VMEM((2, BLK, BLK, 128), jnp.bfloat16),
            VMEM((16, cells), f32),
            pltpu.SemaphoreType.DMA,
        ],
        compiler_params=params,
        name="finish",
    )(*map(close, (local, *x_got, *y_got, *z_got, z_fix, loaded, harm, ids)))
    modes = lax.all_to_all(modes, AXES, 0, 0, tiled=True).sum(0)
    return psi, modes[: 2 * SPHERES, :MODES].reshape(SPHERES, 2, MODES)


def solution(mesh):
    in_specs = (
        P(None, "gx", "gy", "gz"),
        P(None, "gx", "gy", "gz"),
        P("gx", "gy", "gz", None, None),
        P("gx", "gy", "gz", None),
        P(),
        P(),
    )
    out_specs = (P(None, "gx", "gy", "gz"), P())
    return jax.shard_map(shards, mesh=mesh, in_specs=in_specs, out_specs=out_specs, check_vma=False)
```

time: 31.8 us -> 27 us (0.85)
  blocking collectives: 15.8 us -> 12.8 us
  Pallas kernels: 8.51 us -> 6.76 us
    all_to_all x1, blocking collectives: 15.8 us -> 12.8 us  [shards(): modes = lax.all_to_all(modes, AXES, 0, 0, tiled=True).sum(0)]
    pallas_call x1, Pallas kernels: 3.35 us -> 2.2 us  [shards(): pl.pallas_call(interior_kernel, out_shape=[VMEM((2, BLK, BLK, 128), f32),...]
    pallas_call x1, Pallas kernels: 2.66 us -> 2.3 us  [shards(): pl.pallas_call(functools.partial(finish_kernel, slots), out_shape=[pltpu....]
  transfers between devices with their start and end apart: 5 -> 5, of which waited for: 0 -> 0; matrix products, arithmetic and copies ran while one was open for 0% -> 0% of each run, Pallas kernels for 11% -> 8%
where the time goes in v3:
time: 27 us; the launch traced here: 26.8 us
  blocking collectives  12.8 us (47%)
  Pallas kernels  6.76 us (25%)
  starting transfers between devices  5.97 us (22%)
  between operations  0.7 us (3%)
  local copies, waits for them, and re-layouts  0.59 us (2%)
    all_to_all x1, blocking collectives, shards(): modes = lax.all_to_all(modes, AXES, 0, 0, tiled=True).sum(0)  12.8 us
    ppermute x5, starting transfers between devices, swap(): return lax.ppermute(value, AXES, perm)  5.97 us
    pallas_call x1, Pallas kernels, shards(): pl.pallas_call(functools.partial(finish_kernel, slots), out_shape=[pltpu....  2.3 us
    pallas_call x1, Pallas kernels, shards(): pl.pallas_call(functools.partial(faces_kernel, slots), out_shape=[face] *...  2.26 us
    pallas_call x1, Pallas kernels, shards(): pl.pallas_call(interior_kernel, out_shape=[VMEM((2, BLK, BLK, 128), f32),...  2.2 us
    reshape x1, local copies, waits for them, and re-layouts, shards(): return (psi, modes[:2 * SPHERES, :MODES].reshape(SPHERES, 2, MODES))  0.59 us
  transfers between devices with their start and end apart: 5, of which 0 were waited for; matrix products, arithmetic and copies ran while one was open for 0% of the time, Pallas kernels for 8%

profile of v3, /device:TPU:0, one launch (start us, length us, event | category | flops | bytes accessed | tf_op | source)
XLA Modules:
  0.0 26.8 jit_solution(4908366076120168445)
XLA Ops:
  0.6 2.3 %faces.1 = (f32[2,2,16,128]{3,2,1,0:T(8,128)S(1)}, f32[2,2,16,128]{3,2,1,0:T(8,128)S(1)}, f32[2,2,16,128]{3,2,1,0:T(8,128)S(1)}, f32[2,8,128]{2,1,0:T(8,128)S(1)...) custom-call(f32[6,16,16,128]{3,2,1,0:T(8,128)} %metric.1, ...), custom_call_target="tpu_custom_call" | custom-call | tf_op jit(solution)/shard_map/faces/pallas_call | solution.py:519
  2.9 3.0 %collective-permute-start = (f32[2,2,16,128]{3,2,1,0:T(8,128)S(1)}, f32[2,2,16,128]{3,2,1,0:T(8,128)S(1)}, u32[]{:S(2)}, u32[]{:S(2)}) collective-permute-start(f32[2,2,16,128]{3,2,1,0:T(8,128)S(1)} %get-tuple-element.16), channel_id=1, source_target_pairs={{0,16},{1,17},{2,18},{3,19},{4,20},{5,21},{6,22},{7,23},{8,24},{9,... | collective-permute-start | bytes 98312 | tf_op jit(solution)/shard_map/ppermute | solution.py:500
  5.9 0.0 collective-permute-start.1
  5.9 0.2 collective-permute-start.2
  6.1 2.0 %collective-permute-start.3 = (f32[2,8,128]{2,1,0:T(8,128)S(1)}, f32[2,8,128]{2,1,0:T(8,128)S(1)}, u32[]{:S(2)}, u32[]{:S(2)}) collective-permute-start(f32[2,8,128]{2,1,0:T(8,128)S(1)} %get-tuple-element.19), channel_id=1, source_target_pairs={{0,1},{1,0},{2,3},{3,2},{4,5},{5,4},{6,7},{7,6},{8,9},{9,8},{10,11... | collective-permute-start | bytes 24584 | tf_op jit(solution)/shard_map/ppermute | solution.py:500
  8.0 0.8 %collective-permute-start.4 = (f32[2,8,128]{2,1,0:T(8,128)S(1)}, f32[2,8,128]{2,1,0:T(8,128)S(1)}, u32[]{:S(2)}, u32[]{:S(2)}) collective-permute-start(f32[2,8,128]{2,1,0:T(8,128)S(1)} %get-tuple-element.19), channel_id=1, source_target_pairs={{0,4},{1,2},{2,1},{3,7},{4,0},{5,6},{6,5},{7,3},{8,12},{9,10},{10,... | collective-permute-start | bytes 24584 | tf_op jit(solution)/shard_map/ppermute | solution.py:500
  8.9 2.2 %interior.1 = (f32[2,16,16,128]{3,2,1,0:T(8,128)S(1)}, bf16[512,4096]{1,0:T(8,128)(2,1)S(1)}) custom-call(f32[12,20,32,128]{3,2,1,0:T(8,128)S(1)} %get-tuple-element.14.fields, bf16[512,4096]{1,0:T(8,128)(2,1)} %bitcast.5), custom_call_target="tpu_custom_call" | custom-call | flops 20000000 | bytes 8000000 | tf_op jit(solution)/shard_map/interior/pallas_call | solution.py:549
  11.1 0.0 collective-permute-done.3.refs_3_
  11.1 0.0 collective-permute-done.4.refs_4_
  11.1 0.0 collective-permute-done.refs_0_
  11.1 0.0 collective-permute-done.1.refs_1_
  11.1 0.0 collective-permute-done.2.refs_2_
  11.1 2.3 %finish.1 = (bf16[2,16,16,128]{3,2,1,0:T(8,128)(2,1)}, f32[32,8,128]{2,1,0:T(8,128)S(1)}) custom-call(f32[2,16,16,128]{3,2,1,0:T(8,128)S(1)} %get-tuple-element.15.local, f32[2,2,16,128]{3,2,1,0:T(8,128)S(1)} %collective-permute-done.refs_0_, f32[2,2,16,128]{3,2,1,0:T(8,128)S(1)} %collective-permute-done.1.refs_1_, ...), custom_call_target="tpu_custom_call" | custom-call | tf_op jit(solution)/shard_map/finish/pallas_call | solution.py:560
  13.4 12.8 %all_to_all.5 = f32[32,8,128]{2,1,0:T(8,128)S(1)} all-to-all(f32[32,8,128]{2,1,0:T(8,128)S(1)} %get-tuple-element.25), channel_id=1, replica_groups=mesh['gx'=2,'gy'=4,'gz'=4] {'gx','gy','gz'}, dimensions={0} | all-to-all | bytes 262144 | tf_op jit(solution)/shard_map/all_to_all | solution.py:574
  26.2 0.6 %reshape.23 = f32[3,2,77]{2,1,0:T(2,128)} reshape(f32[6,77]{1,0:T(8,128)S(1)} %bitcast.8) | data formatting | bytes 3696 | tf_op jit(solution)/shard_map/reshape | solution.py:575
  (1 shorter events, 0.0 us)
Async XLA Ops:
  2.9 8.2 %collective-permute-start = (f32[2,2,16,128]{3,2,1,0:T(8,128)S(1)}, f32[2,2,16,128]{3,2,1,0:T(8,128)S(1)}, u32[]{:S(2)}, u32[]{:S(2)}) collective-permute-start(f32[2,2,16,128]{3,2,1,0:T(8,128)S(1)} %get-tuple-element.16), channel_id=1, source_target_pairs={{0,16},{1,17},{2,18},{3,19},{4,20},{5,21},{6,22},{7,23},{8,24},{9,... | collective-permute-start | bytes 98312 | tf_op jit(solution)/shard_map/ppermute | solution.py:500
  5.9 5.2 %collective-permute-start.1 = (f32[2,2,16,128]{3,2,1,0:T(8,128)S(1)}, f32[2,2,16,128]{3,2,1,0:T(8,128)S(1)}, u32[]{:S(2)}, u32[]{:S(2)}) collective-permute-start(f32[2,2,16,128]{3,2,1,0:T(8,128)S(1)} %get-tuple-element.17), channel_id=1, source_target_pairs={{0,4},{1,5},{2,6},{3,7},{4,0},{5,1},{6,2},{7,3},{8,12},{9,13},{10,... | collective-permute-start | bytes 98312 | tf_op jit(solution)/shard_map/ppermute | solution.py:500
  5.9 5.2 %collective-permute-start.2 = (f32[2,2,16,128]{3,2,1,0:T(8,128)S(1)}, f32[2,2,16,128]{3,2,1,0:T(8,128)S(1)}, u32[]{:S(2)}, u32[]{:S(2)}) collective-permute-start(f32[2,2,16,128]{3,2,1,0:T(8,128)S(1)} %get-tuple-element.18), channel_id=1, source_target_pairs={{0,16},{1,17},{2,18},{3,19},{4,8},{5,9},{6,10},{7,11},{8,4},{9,5},... | collective-permute-start | bytes 98312 | tf_op jit(solution)/shard_map/ppermute | solution.py:500
  6.1 5.0 %collective-permute-start.3 = (f32[2,8,128]{2,1,0:T(8,128)S(1)}, f32[2,8,128]{2,1,0:T(8,128)S(1)}, u32[]{:S(2)}, u32[]{:S(2)}) collective-permute-start(f32[2,8,128]{2,1,0:T(8,128)S(1)} %get-tuple-element.19), channel_id=1, source_target_pairs={{0,1},{1,0},{2,3},{3,2},{4,5},{5,4},{6,7},{7,6},{8,9},{9,8},{10,11... | collective-permute-start | bytes 24584 | tf_op jit(solution)/shard_map/ppermute | solution.py:500
  8.0 3.0 %collective-permute-start.4 = (f32[2,8,128]{2,1,0:T(8,128)S(1)}, f32[2,8,128]{2,1,0:T(8,128)S(1)}, u32[]{:S(2)}, u32[]{:S(2)}) collective-permute-start(f32[2,8,128]{2,1,0:T(8,128)S(1)} %get-tuple-element.19), channel_id=1, source_target_pairs={{0,4},{1,2},{2,1},{3,7},{4,0},{5,6},{6,5},{7,3},{8,12},{9,10},{10,... | collective-permute-start | bytes 24584 | tf_op jit(solution)/shard_map/ppermute | solution.py:500
